TPU v7x, 256 devices: a whole 4x4x8 slice. The times are simulated.
256 devices in a mesh: dev: 128 (over z, y, x), rep: 2 (over core).
Axes of the slice: x: 4, y: 4, z: 8, core: 2. Of those that a mesh axis runs over, the one named last changes fastest.
Arguments:
- tables: bfloat16 [512, 2048, 128], P('dev'), may hold values from -1.5 to 1.5
- bag_rows: int32 [256, 512, 32, 4], P(('rep', 'dev')), parts along dimension 0, may hold values from 0 to 2047
- bag_lengths: int32 [256, 512, 32], P(('rep', 'dev')), parts along dimension 0, may hold values from 1 to 4
- row_counts: int32 [256, 512], P(('rep', 'dev')), parts along dimension 0, may hold values from 1 to 32, as said below
- inverse: int32 [32768, 512], P(('rep', 'dev')), parts along dimension 0, may hold values from 0 to 31
- table_order: int32 [512], replicated, may hold values from 0 to 511, each once
- compress: bfloat16 [16, 512], replicated, may hold values from -0.25 to 0.25
- top_weight: bfloat16 [8192, 512], replicated, may hold values from -0.0625 to 0.0625
- top_bias: float32 [512], replicated, may hold values from -1.8 to 1.8
Outputs:
- ranked: bfloat16 [32768, 512], P(('rep', 'dev')), parts along dimension 0
There are 2 independent parts, one for each index of `rep`. A program takes and returns all parts, laid end to end along the dimension named above; an argument that names none is the same for every part. Nothing has to cross between parts.
Inputs may be any that keep to these rules, and one draw needn't show every extreme that they name: `row_counts`: for every sample device and every aligned group of 4 consecutive slots the counts sum to at most 80; a count of 32 and a group sum of 80 occur in every draw.
All inputs are finite; a program needn't handle non-finite values.
Results may differ from a plain program's by a relative error of at most 0.0062.
Values may be sent and summed in bfloat16 or wider, within the bound.
A program may use at most 128 MiB of HBM per device.

v0:
```python
import math

import jax
import jax.numpy as jnp
from jax import lax
from jax.sharding import PartitionSpec as P


def pool_bags(tables, bag_ids, bag_lens):
    vocabulary = tables.shape[1]
    table_rows = tables.reshape(-1, tables.shape[2])
    offsets = jnp.arange(tables.shape[0], dtype=jnp.int32) * vocabulary
    wanted = bag_ids + offsets[None, :, None, None]
    picked = jnp.take(table_rows, wanted, axis=0, mode="clip")
    places = jnp.arange(bag_ids.shape[3], dtype=jnp.int32)
    active = places[None, None, None, :] < bag_lens[..., None]
    summed = jnp.sum(jnp.where(active[..., None], picked.astype(jnp.float32), 0.0), axis=3)
    return summed.astype(jnp.bfloat16)


def shards(
    tables, bag_rows, bag_lengths, row_counts, inverse, table_order, compress, top_weight, top_bias
):
    width_emb = tables.shape[2]
    total_slots = table_order.shape[0]
    most_rows = bag_rows.shape[2]
    my_counts = row_counts[0]
    got_rows, got_lengths = (
        lax.all_to_all(bag_rows, "dev", split_axis=1, concat_axis=0, tiled=True),
        lax.all_to_all(bag_lengths, "dev", split_axis=1, concat_axis=0, tiled=True),
    )
    pooled = pool_bags(tables, got_rows, got_lengths)
    arrived = lax.all_to_all(pooled, "dev", split_axis=0, concat_axis=1, tiled=True).reshape(
        -1, width_emb
    )
    slot_base = jnp.arange(total_slots, dtype=jnp.int32) * most_rows
    slot_range = jnp.arange(total_slots, dtype=jnp.int32)
    matches = table_order[:, None] == slot_range[None, :]
    feature_base = jnp.sum(jnp.where(matches, slot_base[:, None], 0), axis=0)
    feature_count = jnp.sum(jnp.where(matches, my_counts[:, None], 0), axis=0)
    row_range = jnp.arange(most_rows, dtype=jnp.int32)
    feature_rows = jnp.take(
        arrived, feature_base[:, None] + row_range[None, :], axis=0, mode="clip"
    )
    samples = inverse.shape[0]
    block_rows = math.gcd(samples, 128)

    def score_block(inverse_block):
        present = inverse_block < feature_count[None, :]
        selector = (inverse_block[..., None] == row_range[None, None, :]) & present[..., None]
        selector = selector.astype(jnp.bfloat16)
        features = jnp.einsum(
            "bfu,fue->bfe", selector, feature_rows, preferred_element_type=jnp.float32
        ).astype(jnp.bfloat16)
        mixed = jnp.einsum(
            "kf,bfe->bke", compress, features, preferred_element_type=jnp.float32
        ).astype(jnp.bfloat16)
        pairwise = jnp.einsum(
            "bfe,bke->bfk", features, mixed, preferred_element_type=jnp.float32
        ).astype(jnp.bfloat16)
        hidden_pre = (
            jnp.dot(
                pairwise.reshape(pairwise.shape[0], -1),
                top_weight,
                preferred_element_type=jnp.float32,
            )
            + top_bias
        )
        return jnp.maximum(hidden_pre, 0.0).astype(jnp.bfloat16)

    ranked = lax.map(score_block, inverse.reshape(samples // block_rows, block_rows, total_slots))
    return ranked.reshape(samples, -1)


def solution(mesh):
    return jax.shard_map(
        shards,
        mesh=mesh,
        in_specs=(
            P("dev", None, None),
            P(("rep", "dev"), None, None, None),
            P(("rep", "dev"), None, None),
            P(("rep", "dev"), None),
            P(("rep", "dev"), None),
            P(),
            P(),
            P(),
            P(),
        ),
        out_specs=P(("rep", "dev"), None),
        check_vma=False,
    )
```

profile of v0, /device:TPU:8, one launch (start us, length us, event | category | flops | bytes accessed | tf_op | source)
XLA Modules:
  0.0 546.5 jit_solution(15885233483454164998)
XLA Ops:
  0.0 1.1 copy.39
  1.7 1.3 reduce.1
  3.0 0.8 reshape.111
  3.8 15.3 %all-to-all-start = ((s32[128,1,128]{2,1,0:T(1,128)}), s32[128,1,128]{2,1,0:T(1,128)S(1)}, u32[]{:S(2)}, u32[]{:S(2)}) async-start(s32[128,1,128]{2,1,0:T(1,128)} %reshape.111), calls=%async_computation | async-start | bytes 131072 | tf_op jit(solution)/shard_map/all_to_all | solution.py:30
  19.1 1.4 copy.40
  20.5 1.4 reshape.109
  21.8 8.6 %all-to-all-done = s32[128,1,128]{2,1,0:T(1,128)S(1)} async-done(((s32[128,1,128]{2,1,0:T(1,128)}), s32[128,1,128]{2,1,0:T(1,128)S(1)}, u32[]{:S(2)}, u32[]{:S(2)}) %all-to-all-start) | async-done | bytes 65568 | tf_op jit(solution)/shard_map/all_to_all | solution.py:30
  30.4 6.6 %all-to-all-start.1 = ((s32[128,1,512]{2,1,0:T(1,128)}), s32[128,1,512]{2,1,0:T(1,128)S(1)}, u32[]{:S(2)}, u32[]{:S(2)}) async-start(s32[128,1,512]{2,1,0:T(1,128)} %reshape.109), calls=%async_computation.1 | async-start | bytes 524288 | tf_op jit(solution)/shard_map/all_to_all | solution.py:29
  37.1 0.8 reduce.2
  38.3 4.6 iota_compare_fusion.1
  42.9 7.7 %all-to-all-done.1 = s32[128,1,512]{2,1,0:T(1,128)S(1)} async-done(((s32[128,1,512]{2,1,0:T(1,128)}), s32[128,1,512]{2,1,0:T(1,128)S(1)}, u32[]{:S(2)}, u32[]{:S(2)}) %all-to-all-start.1) | async-done | bytes 262176 | tf_op jit(solution)/shard_map/all_to_all | solution.py:29
  50.6 1.2 reduce
  52.7 5.2 copy.42
  57.9 8.2 %reshape.91 = s32[65536]{0:T(1024)S(1)} reshape(s32[128,4,32,4,1]{3,2,1,0,4:T(8,128)} %copy.42) | data formatting | bytes 524288 | tf_op jit(solution)/shard_map/add | solution.py:13
  66.1 227.3 %gather_fusion = bf16[65536,128]{1,0:T(8,128)(2,1)} fusion(bf16[8192,128]{1,0:T(8,128)(2,1)S(1)} %bitcast.30, s32[65536]{0:T(1024)S(1)} %broadcast_clamp_fusion), kind=kCustom, calls=%fused_computation | custom fusion | bytes 33816576 | tf_op jit(solution)/shard_map/jit(_take)/gather | solution.py:14
  293.5 35.9 %fusion = bf16[128,4,32,128]{3,2,1,0:T(8,128)(2,1)} fusion(bf16[128,4,32,4,128]{4,3,2,1,0:T(4,128)(2,1)} %bitcast.31, pred[128,4,32,4]{3,2,1,0:T(8,128)(4,1)} %iota_compare_fusion.1), kind=kLoop, calls=%fused_computation.3 | loop fusion | flops 23068672 | bytes 21037056 | tf_op jit(solution)/shard_map/reduce_sum | solution.py:17
  329.4 7.9 %all-to-all-start.2 = ((bf16[128,4,32,128]{3,2,1,0:T(8,128)(2,1)}), bf16[128,4,32,128]{3,2,1,0:T(8,128)(2,1)}, u32[]{:S(2)}, u32[]{:S(2)}) async-start(bf16[128,4,32,128]{3,2,1,0:T(8,128)(2,1)} %fusion), calls=%async_computation.2 | async-start | bytes 8388608 | tf_op jit(solution)/shard_map/all_to_all | solution.py:33
  338.3 92.4 %all-to-all-done.2 = bf16[128,4,32,128]{3,2,1,0:T(8,128)(2,1)} async-done(((bf16[128,4,32,128]{3,2,1,0:T(8,128)(2,1)}), bf16[128,4,32,128]{3,2,1,0:T(8,128)(2,1)}, u32[]{:S(2)}, u32[]{:S(2)}) %all-to-all-start.2) | async-done | bytes 4194336 | tf_op jit(solution)/shard_map/all_to_all | solution.py:33
  430.7 57.6 %gather_fusion.1 = bf16[16384,128]{1,0:T(8,128)(2,1)} fusion(bf16[16384,128]{1,0:T(8,128)(2,1)} %bitcast.4, s32[16384]{0:T(1024)S(1)} %broadcast_clamp_fusion.1), kind=kCustom, calls=%fused_computation.1 | custom fusion | bytes 8454144 | tf_op jit(solution)/shard_map/jit(_take)/gather | solution.py:42
  488.3 9.8 %convert_bitcast_fusion = bf16[128,512,128]{0,2,1:T(8,128)(2,1)} fusion(bf16[512,32,128]{2,1,0:T(8,128)(2,1)} %bitcast.32, s32[128,512]{0,1:T(8,128)S(1)} %copy.43, pred[128,512]{0,1:T(8,128)(4,1)S(1)} %copy.44), kind=kOutput, calls=%fused_computation.4 | convolution fusion | flops 549453824 | bytes 21299200 | tf_op jit(solution)/shard_map/while/body/eval_jaxpr/bfu,fue->bfe/dot_general | solution.py:52
  498.1 21.5 %copy.46 = bf16[128,512,128]{2,1,0:T(8,128)(2,1)} copy(bf16[128,512,128]{0,2,1:T(8,128)(2,1)} %convert_bitcast_fusion) | data formatting | bytes 33554432 | tf_op jit(solution)/shard_map/while/body/eval_jaxpr/convert_element_type | solution.py:54
  519.6 16.9 %convolution_convert_fusion = bf16[128,512,16]{1,2,0:T(8,128)(2,1)S(1)} fusion(bf16[128,512,128]{2,1,0:T(8,128)(2,1)} %copy.46, bf16[16,512]{1,0:T(8,128)(2,1)S(1)} %copy-done.3), kind=kOutput, calls=%fused_computation.10 | convolution fusion | flops 538181632 | bytes 18890752 | tf_op jit(solution)/shard_map/while/body/eval_jaxpr/bfe,bke->bfk/dot_general | solution.py:58
  536.4 3.9 copy.47
  540.4 6.1 %fusion.6 = bf16[128,512]{1,0:T(8,128)(2,1)} fusion(bf16[128,8192]{0,1:T(8,128)(2,1)} %bitcast.33, bf16[8192,512]{1,0:T(8,128)(2,1)} %param.16, f32[512]{0:T(512)S(1)} %copy-done.4), kind=kOutput, calls=%fused_computation.14 | convolution fusion | flops 1073938432 | bytes 10618880 | tf_op jit(solution)/shard_map/while/body/eval_jaxpr/dot_general | solution.py:62
  (29 shorter events, 2.8 us)
Async XLA Ops:
  0.0 66.1 %copy-start = (bf16[4,2048,128]{2,1,0:T(8,128)(2,1)S(1)}, bf16[4,2048,128]{2,1,0:T(8,128)(2,1)}, u32[]{:S(2)}) copy-start(bf16[4,2048,128]{2,1,0:T(8,128)(2,1)} %param.9) | copy-start | bytes 6291460
  3.8 26.6 %all-to-all-start = ((s32[128,1,128]{2,1,0:T(1,128)}), s32[128,1,128]{2,1,0:T(1,128)S(1)}, u32[]{:S(2)}, u32[]{:S(2)}) async-start(s32[128,1,128]{2,1,0:T(1,128)} %reshape.111), calls=%async_computation | async-start | bytes 131072 | tf_op jit(solution)/shard_map/all_to_all | solution.py:30
  30.4 20.2 %all-to-all-start.1 = ((s32[128,1,512]{2,1,0:T(1,128)}), s32[128,1,512]{2,1,0:T(1,128)S(1)}, u32[]{:S(2)}, u32[]{:S(2)}) async-start(s32[128,1,512]{2,1,0:T(1,128)} %reshape.109), calls=%async_computation.1 | async-start | bytes 524288 | tf_op jit(solution)/shard_map/all_to_all | solution.py:29
  329.4 7.9 %copy-start.2 = (s32[128,512]{1,0:T(8,128)S(1)}, s32[128,512]{1,0:T(8,128)}, u32[]{:S(2)}) copy-start(s32[128,512]{1,0:T(8,128)} %param.13) | copy-start | bytes 786436
  329.4 8.1 %copy-start.5 = (s32[1,512]{1,0:T(1,128)S(1)}, s32[1,512]{1,0:T(1,128)}, u32[]{:S(2)}) copy-start(s32[1,512]{1,0:T(1,128)} %param.12) | copy-start | bytes 6148
  329.4 8.1 %copy-start.6 = (s32[512]{0:T(512)S(1)}, s32[512]{0:T(512)}, u32[]{:S(2)}) copy-start(s32[512]{0:T(512)} %param.14) | copy-start | bytes 6148
  329.4 101.3 %all-to-all-start.2 = ((bf16[128,4,32,128]{3,2,1,0:T(8,128)(2,1)}), bf16[128,4,32,128]{3,2,1,0:T(8,128)(2,1)}, u32[]{:S(2)}, u32[]{:S(2)}) async-start(bf16[128,4,32,128]{3,2,1,0:T(8,128)(2,1)} %fusion), calls=%async_computation.2 | async-start | bytes 8388608 | tf_op jit(solution)/shard_map/all_to_all | solution.py:33
  498.1 21.5 %copy-start.3 = (bf16[16,512]{1,0:T(8,128)(2,1)S(1)}, bf16[16,512]{1,0:T(8,128)(2,1)}, u32[]{:S(2)}) copy-start(bf16[16,512]{1,0:T(8,128)(2,1)} %param.15) | copy-start | bytes 49156
  519.6 20.8 %copy-start.4 = (f32[512]{0:T(512)S(1)}, f32[512]{0:T(512)}, u32[]{:S(2)}) copy-start(f32[512]{0:T(512)} %param.17) | copy-start | bytes 6148
  540.4 6.1 %copy-start.1 = (bf16[4,2048,128]{2,1,0:T(8,128)(2,1)S(1)}, bf16[4,2048,128]{2,1,0:T(8,128)(2,1)}, u32[]{:S(2)}) copy-start(bf16[4,2048,128]{2,1,0:T(8,128)(2,1)} %param.9) | copy-start | bytes 6291460
where the time goes:
time: 547 us; the launch traced here: 546 us
  local copies, waits for them, and re-layouts  330 us (60%)
  waiting for transfers between devices  109 us (20%)
  other arithmetic  44.5 us (8%)
  matrix products  32.8 us (6%)
  starting transfers between devices  29.9 us (5%)
    gather x1, local copies, waits for them, and re-layouts, pool_bags(): picked = jnp.take(table_rows, wanted, axis=0, mode='clip')  227 us
    all_to_all x1, waiting for transfers between devices, shards(): lax.all_to_all(pooled, 'dev', split_axis=0, concat_axis=1, tiled=True)  92.4 us
    gather x1, local copies, waits for them, and re-layouts, shards(): jnp.take(arrived, feature_base[:, None] + row_range[None, :], axis=0, mod...  57.6 us
    reduce_sum x1, other arithmetic, pool_bags(): jnp.sum(jnp.where(active[..., None], picked.astype(jnp.float32), 0.0), ax...  35.9 us
    convert_element_type x1, local copies, waits for them, and re-layouts, score_block(): features = jnp.einsum('bfu,fue->bfe', selector, feature_rows, preferred_e...  21.5 us
    dot_general x1, matrix products, score_block(): jnp.einsum('bfe,bke->bfk', features, mixed, preferred_element_type=jnp.fl...  16.9 us
    all_to_all x1, starting transfers between devices, shards(): lax.all_to_all(bag_lengths, 'dev', split_axis=1, concat_axis=0, tiled=True)  15.3 us
    add x2, local copies, waits for them, and re-layouts, pool_bags(): wanted = bag_ids + offsets[None, :, None, None]  13.4 us
  transfers between devices with their start and end apart: 3, of which 3 were waited for; matrix products, arithmetic and copies ran while one was open for 2% of the time, Pallas kernels for 0%

commit v1 on v0

v1 whole, which is shorter than its diff:
```python
import functools
import jax
import jax.numpy as jnp
from jax import lax
from jax.experimental import pallas as pl
from jax.experimental.pallas import tpu as pltpu
from jax.sharding import PartitionSpec as P

BF = jnp.bfloat16
F32 = jnp.float32
I32 = jnp.int32
ROOM = 80


def iota(shape, axis):
    return lax.broadcasted_iota(I32, shape, axis)


def onehot(mask):
    return jnp.where(mask, 1.0, 0.0).astype(BF)


def prep_body(rows_ref, lens_ref, counts_ref, out_ref):
    most, pool, slots = rows_ref.shape
    used = iota((most, slots), 0) < counts_ref[...]
    lens = lens_ref[...]
    parts = [
        jnp.where(used & (p < lens), rows_ref[:, p, :], -1) for p in range(pool)
    ]
    wide = jnp.concatenate(parts, axis=0)
    for at in range(slots // 128):
        out_ref[pl.ds(at * 128, 128), :] = wide[:, at * 128 : (at + 1) * 128].T


def pool_setup(tables_ref, ids_ref, turned_ref, y_ref, pos_ref):
    tabs, vocab, width = tables_ref.shape
    for j in range(tabs):
        for at in range(vocab // 128):
            turned_ref[j, :, pl.ds(at * 128, 128)] = tables_ref[
                j, pl.ds(at * 128, 128), :
            ].astype(F32).T.astype(BF)
    lane = iota((32, 128), 1)
    chunk = lane // 32
    same = onehot(iota((128, 128), 0) // 32 == iota((128, 128), 1) // 32)
    base = jnp.zeros((32, 128), F32)
    for j in range(4):
        got = [ids_ref[pl.ds(4 * q + j, 32, stride=16), :] for q in range(4)]
        for p in range(4):
            y = got[0] if p == 0 else pltpu.roll(got[0], (-p * 32) % 128, 1)
            for q in range(1, 4):
                moved = got[q] if p == q else pltpu.roll(got[q], ((q - p) * 32) % 128, 1)
                y = jnp.where(chunk == q, moved, y)
            y_ref[pl.ds((j * 4 + p) * 32, 32), :] = y
            if p == 0:
                valid = y >= 0
                total = jnp.dot(onehot(valid), same, preferred_element_type=F32)
                place = base.astype(I32) + (lane % 32) + chunk * ROOM
                pos_ref[pl.ds(j * 32, 32), :] = jnp.where(valid, place, -1)
                base = base + total


def pool_pair(t, turned_ref, y_ref, pos_ref, hot_ref, xt_ref):
    width = turned_ref.shape[1]
    low_iota = iota((128, 128), 0)

    def table(j, carry):
        for half in range(2):
            lows, highs = [], []
            for p in range(4):
                y = y_ref[pl.ds((j * 4 + p) * 32 + 2 * t + half, 1), :]
                lows.append(onehot(jnp.broadcast_to(y & 127, (128, 128)) == low_iota))
                highs.append(jnp.broadcast_to(y >> 7, (16, 128)))
            for h in range(16):
                pick = [onehot(high == h) for high in highs]
                for at in range(8):
                    cut = [low[at * 16 : at * 16 + 16, :] for low in lows]
                    hot_ref[
                        pl.ds(h * 128 + at * 16, 16), half * 128 : half * 128 + 128
                    ] = (cut[0] * pick[0] + cut[1] * pick[1]) + (
                        cut[2] * pick[2] + cut[3] * pick[3]
                    )
        pooled = jnp.dot(
            turned_ref[j], hot_ref[...], preferred_element_type=F32
        ).astype(BF)
        xt_ref[0, j] = pooled[:, :128]
        xt_ref[1, j] = pooled[:, 128:]
        return carry

    lax.fori_loop(0, 4, table, 0)
    out = []
    for half in range(2):
        total = None
        for jj in range(2):
            packs, cols = [], []
            for j in (2 * jj, 2 * jj + 1):
                pos = pos_ref[pl.ds(j * 32 + 2 * t + half, 1), :]
                packs.append(
                    onehot(
                        jnp.broadcast_to(pos, (4 * ROOM, 128)) == iota((4 * ROOM, 128), 0)
                    )
                )
                cols.append(xt_ref[half, j])
            part = lax.dot_general(
                jnp.concatenate(packs, axis=1),
                jnp.concatenate(cols, axis=1),
                (((1,), (1,)), ((), ())),
                preferred_element_type=F32,
            )
            total = part if total is None else total + part
        out.append(total.astype(BF))
    return out


def pool_body(tables_ref, ids_ref, out_ref, turned_ref, y_ref, pos_ref, hot_ref, xt_ref):
    pool_setup(tables_ref, ids_ref, turned_ref, y_ref, pos_ref)

    def step(t, carry):
        blocks = pool_pair(t, turned_ref, y_ref, pos_ref, hot_ref, xt_ref)
        for half in range(2):
            out_ref[pl.ds(pl.multiple_of((2 * t + half) * 4 * ROOM, 4 * ROOM), 4 * ROOM), :] = blocks[half]
        return carry

    lax.fori_loop(0, 16, step, 0)


def pool_scratch():
    return [
        pltpu.VMEM((4, 128, 2048), BF),
        pltpu.VMEM((512, 128), I32),
        pltpu.VMEM((128, 128), I32),
        pltpu.VMEM((2048, 256), BF),
        pltpu.VMEM((2, 4, 128, 128), BF),
    ]


def order_columns(order_ref):
    slots = order_ref.shape[1]
    return onehot(iota((slots, slots), 0) == order_ref[...])


def weight_body(order_ref, top_ref, out_ref, plane_ref):
    slots, units = out_ref.shape[1:]
    row = iota((256, 256), 0)
    col = iota((256, 256), 1)
    spread = onehot((col % 16 == row // 16) & (col // 16 == row % 16))

    def cut(at, carry):
        block = jnp.dot(
            spread, top_ref[pl.ds(pl.multiple_of(at * 256, 256), 256), :], preferred_element_type=F32
        ).astype(BF)
        for k in range(16):
            plane_ref[k, pl.ds(pl.multiple_of(at * 16, 16), 16), :] = block[k * 16 : k * 16 + 16, :]
        return carry

    lax.fori_loop(0, slots // 16, cut, 0)
    perm = order_columns(order_ref).astype(F32).T.astype(BF)

    def turn(k, carry):
        out_ref[k] = jnp.dot(perm, plane_ref[k], preferred_element_type=F32).astype(BF)
        return carry

    lax.fori_loop(0, 16, turn, 0)


def target_setup(inverse_ref, counts_ref, order_ref, compress_ref, turn_ref, mix_ref):
    samples, slots = inverse_ref.shape
    columns = order_columns(order_ref)
    mix_ref[...] = jnp.dot(compress_ref[...], columns, preferred_element_type=F32).astype(BF)
    chosen = jnp.dot(inverse_ref[...].astype(F32).astype(BF), columns, preferred_element_type=F32)
    counts = jnp.broadcast_to(counts_ref[...], (16, slots)).astype(F32)
    before = (iota((slots, slots), 0) // 4 == iota((slots, slots), 1) // 4) & (
        iota((slots, slots), 0) < iota((slots, slots), 1)
    )
    base = jnp.dot(counts.astype(BF), onehot(before), preferred_element_type=F32)[:1, :]
    offset = ((iota((1, slots), 1) // 4) % 2 * ROOM).astype(F32)
    place = jnp.where(chosen < counts[:1, :], chosen + (base + offset), -1.0)
    for at in range(slots // 128):
        turn_ref[pl.ds(at * 128, 128), :] = place[:, at * 128 : (at + 1) * 128].T


def pick_half(slot, rows, turn_ref, lhs_ref):
    place = turn_ref[pl.ds(pl.multiple_of(slot, 8), 8), :]
    lanes = iota((8, 128), 1).astype(F32)
    for b in range(0, 128, 2):
        left = [jnp.broadcast_to(place[:, b + i : b + i + 1], (8, 128)) for i in range(2)]
        near = jnp.concatenate([jnp.where(x == lanes, 1.0, 0.0) for x in left], axis=0)
        far = jnp.concatenate([jnp.where(x == lanes + 128.0, 1.0, 0.0) for x in left], axis=0)
        lhs_ref[b * 8 : b * 8 + 16, 0:128] = near.astype(BF)
        lhs_ref[b * 8 : b * 8 + 16, 128:256] = far.astype(BF)
    return jnp.dot(lhs_ref[:, :160], rows, preferred_element_type=F32)


def pick_chunk(c, packed_ref, turn_ref, lhs_ref, feat_ref):
    halves = []
    for half in range(2):
        rows = packed_ref[pl.ds(pl.multiple_of(c * 320 + half * 160, 160), 160), :]
        halves.append(pick_half(c * 16 + half * 8, rows, turn_ref, lhs_ref).reshape(128, 8, 128))
    both = jnp.concatenate(halves, axis=1).astype(BF).reshape(64, 2, 16, 128)
    at = pl.ds(pl.multiple_of(c * 16, 16), 16)
    feat_ref[:, at, 0:128] = both[:, 0]
    feat_ref[:, at, 128:256] = both[:, 1]


def finish(feat_ref, mix_ref, weight_ref, bias_ref, out_ref, pair_ref, acc_ref):
    mix = mix_ref[...]
    zero = jnp.zeros((16, 128), BF)

    def pair(i, carry):
        feats = feat_ref[i]
        mixed = jnp.dot(mix, feats, preferred_element_type=F32).astype(BF)
        lhs = jnp.concatenate(
            [
                jnp.concatenate([mixed[:, :128], zero], axis=1),
                jnp.concatenate([zero, mixed[:, 128:]], axis=1),
            ],
            axis=0,
        )
        both = lax.dot_general(
            lhs, feats, (((1,), (1,)), ((), ())), preferred_element_type=F32
        )
        for at in range(4):
            pair_ref[at, pl.ds(pl.multiple_of(i * 32, 32), 32), :] = both[:, at * 128 : at * 128 + 128]
        return carry

    lax.fori_loop(0, feat_ref.shape[0], pair, 0)
    acc_ref[...] = jnp.broadcast_to(bias_ref[...], acc_ref.shape)

    def plane(k, carry):
        lhs = jnp.concatenate(
            [pair_ref[at, pl.ds(k, 128, stride=16), :].astype(BF) for at in range(4)], axis=1
        )
        acc_ref[...] += jnp.dot(lhs, weight_ref[k], preferred_element_type=F32)
        return carry

    lax.fori_loop(0, 16, plane, 0)
    out_ref[...] = jnp.maximum(acc_ref[...], 0.0).astype(BF)


def score_body(
    packed_ref, inverse_ref, counts_ref, order_ref, compress_ref, weight_ref, bias_ref,
    out_ref, turn_ref, mix_ref, lhs_ref, feat_ref, pair_ref, acc_ref,
):
    target_setup(inverse_ref, counts_ref, order_ref, compress_ref, turn_ref, mix_ref)

    def chunk(c, carry):
        pick_chunk(c, packed_ref, turn_ref, lhs_ref, feat_ref)
        return carry

    lax.fori_loop(0, 32, chunk, 0)
    finish(feat_ref, mix_ref, weight_ref, bias_ref, out_ref, pair_ref, acc_ref)


def score_scratch():
    return [
        pltpu.VMEM((512, 128), F32),
        pltpu.VMEM((16, 512), BF),
        pltpu.VMEM((1024, 256), BF),
        pltpu.VMEM((64, 512, 256), BF),
        pltpu.VMEM((4, 2048, 128), F32),
        pltpu.VMEM((128, 512), F32),
    ]


VM = pl.BlockSpec(memory_space=pltpu.VMEM)
BIG = 60 * 1024 * 1024


def call(body, outs, scratch, count, flops, **kw):
    return pl.pallas_call(
        body,
        out_shape=outs,
        in_specs=[VM] * count,
        out_specs=VM,
        scratch_shapes=scratch,
        compiler_params=pltpu.CompilerParams(vmem_limit_bytes=BIG, **kw),
        cost_estimate=pl.CostEstimate(flops=flops, bytes_accessed=4 << 20, transcendentals=0),
    )


def shards(tables, bag_rows, bag_lengths, row_counts, inverse, table_order, compress, top_weight, top_bias):
    order = table_order.reshape(1, -1)
    bias = top_bias.reshape(1, -1)
    slots = table_order.shape[0]
    rows = bag_rows[0].transpose(1, 2, 0)
    lens = bag_lengths[0].transpose(1, 0)
    ids = call(prep_body, jax.ShapeDtypeStruct((slots, 128), I32), [], 3, 10**6)(rows, lens, row_counts)
    got = lax.all_to_all(ids.reshape(128, 4, 128), "dev", split_axis=0, concat_axis=0, tiled=True)
    packed = call(pool_body, jax.ShapeDtypeStruct((128 * ROOM, 128), BF), pool_scratch(), 2, 9 * 10**9)(
        tables, got.reshape(512, 128)
    )
    arrived = lax.all_to_all(packed.reshape(128, ROOM, 128), "dev", split_axis=0, concat_axis=0, tiled=True)
    weight = call(
        weight_body,
        jax.ShapeDtypeStruct((16, slots, 512), BF),
        [pltpu.VMEM((16, slots, 512), BF)],
        2,
        6 * 10**9,
    )(order, top_weight)
    return call(score_body, jax.ShapeDtypeStruct((128, 512), BF), score_scratch(), 7, 10**10)(
        arrived.reshape(128 * ROOM, 128), inverse, row_counts, order, compress, weight, bias
    )


def solution(mesh):
    return jax.shard_map(
        shards,
        mesh=mesh,
        in_specs=(
            P("dev", None, None),
            P(("rep", "dev"), None, None, None),
            P(("rep", "dev"), None, None),
            P(("rep", "dev"), None),
            P(("rep", "dev"), None),
            P(),
            P(),
            P(),
            P(),
        ),
        out_specs=P(("rep", "dev"), None),
        check_vma=False,
    )
```

time: 547 us -> 208 us (0.38)
  local copies, waits for them, and re-layouts: 330 us -> 1.57 us
  Pallas kernels: 0 us -> 129 us
  waiting for transfers between devices: 109 us -> 40.7 us
  other arithmetic: 44.5 us -> 0 us
  matrix products: 32.8 us -> 0 us
  blocking collectives: 0 us -> 30.1 us
  starting transfers between devices: 29.9 us -> 6.64 us
    gather x2 -> x0, local copies, waits for them, and re-layouts: 285 us -> none  [the longest x1 227 us: pool_bags(): picked = jnp.take(table_rows, wanted, axis=0, mode='clip')]
    pallas_call x0 -> x4, Pallas kernels: none -> 129 us  [the longest x1 57.8 us: shards(): call(pool_body, jax.ShapeDtypeStruct((128 * ROOM, 128), BF), pool_scratch...]
    all_to_all x3 -> x1, waiting for transfers between devices: 109 us -> 40.7 us  [shards(): lax.all_to_all(packed.reshape(128, ROOM, 128), 'dev', split_axis=0, conca...]
    reduce_sum x2 -> x0, other arithmetic: 36.2 us -> none  [the longest x1 35.9 us: pool_bags(): jnp.sum(jnp.where(active[..., None], picked.astype(jnp.float32), 0.0), ax...]
    dot_general x3 -> x0, matrix products: 32.8 us -> none  [the longest x1 16.9 us: score_block(): jnp.einsum('bfe,bke->bfk', features, mixed, preferred_element_type=jnp.fl...]
    all_to_all x0 -> x1, blocking collectives: none -> 30.1 us  [shards(): lax.all_to_all(ids.reshape(128, 4, 128), 'dev', split_axis=0, concat_axis...]
    convert_element_type x2 -> x0, local copies, waits for them, and re-layouts: 25.4 us -> none  [the longest x1 21.5 us: score_block(): features = jnp.einsum('bfu,fue->bfe', selector, feature_rows, preferred_e...]
    all_to_all x3 -> x1, starting transfers between devices: 29.9 us -> 6.64 us  [shards(): lax.all_to_all(packed.reshape(128, ROOM, 128), 'dev', split_axis=0, conca...]
  transfers between devices with their start and end apart: 3 -> 1, of which waited for: 3 -> 1; matrix products, arithmetic and copies ran while one was open for 2% -> 0% of each run, Pallas kernels for 0% -> 10%
where the time goes in v1:
time: 208 us
  Pallas kernels  129 us (62%)
  waiting for transfers between devices  40.7 us (20%)
  blocking collectives  30.1 us (14%)
  starting transfers between devices  6.64 us (3%)
    pallas_call x1, Pallas kernels, shards(): call(pool_body, jax.ShapeDtypeStruct((128 * ROOM, 128), BF), pool_scratch...  57.8 us
    pallas_call x1, Pallas kernels, shards(): call(score_body, jax.ShapeDtypeStruct((128, 512), BF), score_scratch(), 7...  47.9 us
    all_to_all x1, waiting for transfers between devices, shards(): lax.all_to_all(packed.reshape(128, ROOM, 128), 'dev', split_axis=0, conca...  40.7 us
    all_to_all x1, blocking collectives, shards(): lax.all_to_all(ids.reshape(128, 4, 128), 'dev', split_axis=0, concat_axis...  30.1 us
    pallas_call x1, Pallas kernels, shards(): call(weight_body, jax.ShapeDtypeStruct((16, slots, 512), BF), [pltpu.VMEM...  21.4 us
    all_to_all x1, starting transfers between devices, shards(): lax.all_to_all(packed.reshape(128, ROOM, 128), 'dev', split_axis=0, conca...  6.64 us
  transfers between devices with their start and end apart: 1, of which 1 were waited for; matrix products, arithmetic and copies ran while one was open for 0% of the time, Pallas kernels for 10%

profile of v1, /device:TPU:8, one launch (start us, length us, event | category | flops | bytes accessed | tf_op | source)
XLA Modules:
  0.0 208.0 jit_solution(1477005152300256193)
XLA Ops:
  0.0 1.9 shard_map.91
  1.9 30.1 %all_to_all.10 = s32[128,4,128]{2,1,0:T(4,128)} all-to-all(s32[128,4,128]{2,1,0:T(4,128)} %bitcast.14), channel_id=1, replica_groups=mesh['dev'=128,'rep'=2] {'dev'}, dimensions={0} | all-to-all | bytes 524288 | tf_op jit(solution)/shard_map/all_to_all | solution.py:287
  31.9 57.8 %shard_map.92 = bf16[10240,128]{1,0:T(8,128)(2,1)} custom-call(bf16[4,2048,128]{2,1,0:T(8,128)(2,1)} %tables_ref.1, s32[512,128]{1,0:T(8,128)} %bitcast.16), custom_call_target="tpu_custom_call" | custom-call | flops 8999999488 | bytes 4194304 | tf_op jit(solution)/shard_map/pallas_call | solution.py:288
  89.7 6.6 %all-to-all-start.1 = ((bf16[128,80,128]{2,1,0:T(8,128)(2,1)}), bf16[128,80,128]{2,1,0:T(8,128)(2,1)S(1)}, u32[]{:S(2)}, u32[]{:S(2)}) async-start(bf16[128,80,128]{2,1,0:T(8,128)(2,1)} %bitcast.13), calls=%async_computation.1 | async-start | bytes 5242880 | tf_op jit(solution)/shard_map/all_to_all | solution.py:291
  96.4 21.4 %shard_map.93.weight_ref = bf16[16,512,512]{2,1,0:T(8,128)(2,1)} custom-call(s32[1,512]{1,0:T(1,128)} %bitcast.18, bf16[8192,512]{1,0:T(8,128)(2,1)} %top_ref.1), custom_call_target="tpu_custom_call" | custom-call | flops 6000000000 | bytes 4194304 | tf_op jit(solution)/shard_map/pallas_call | solution.py:292
  117.8 40.7 %all-to-all-done.1 = bf16[128,80,128]{2,1,0:T(8,128)(2,1)S(1)} async-done(((bf16[128,80,128]{2,1,0:T(8,128)(2,1)}), bf16[128,80,128]{2,1,0:T(8,128)(2,1)S(1)}, u32[]{:S(2)}, u32[]{:S(2)}) %all-to-all-start.1) | async-done | bytes 2621472 | tf_op jit(solution)/shard_map/all_to_all | solution.py:291
  158.5 0.0 copy-start
  158.5 1.6 copy-done
  160.1 47.9 %shard_map.94 = bf16[128,512]{1,0:T(8,128)(2,1)} custom-call(bf16[10240,128]{1,0:T(8,128)(2,1)} %bitcast.12, s32[128,512]{1,0:T(8,128)} %inverse_ref.1, s32[1,512]{1,0:T(1,128)} %counts_ref.3, s32[1,512]{1,0:T(1,128)} %bitcast.19, bf16[16,512]{1,0:T(8,128)(2,1)} %compress_ref.1, bf16[16,512,512]{2,1,0:T(8,128)(2,1)} %shard_map.93.weight_ref, f32[1,512]{1,0:T(1,128)} %bitcast.20), custom_call_target="tpu_custom_call" | custom-call | flops 10000000000 | bytes 4194304 | tf_op jit(solution)/shard_map/pallas_call | solution.py:299
Async XLA Ops:
  89.7 68.8 %all-to-all-start.1 = ((bf16[128,80,128]{2,1,0:T(8,128)(2,1)}), bf16[128,80,128]{2,1,0:T(8,128)(2,1)S(1)}, u32[]{:S(2)}, u32[]{:S(2)}) async-start(bf16[128,80,128]{2,1,0:T(8,128)(2,1)} %bitcast.13), calls=%async_computation.1 | async-start | bytes 5242880 | tf_op jit(solution)/shard_map/all_to_all | solution.py:291
  158.5 1.6 copy-start

commit v2 on v1

v2 whole, which is shorter than its diff:
```python
import functools
import jax
import jax.numpy as jnp
from jax import lax
from jax.experimental import pallas as pl
from jax.experimental.pallas import tpu as pltpu
from jax.sharding import PartitionSpec as P

BF = jnp.bfloat16
F32 = jnp.float32
I32 = jnp.int32
ROOM = 80


def iota(shape, axis):
    return lax.broadcasted_iota(I32, shape, axis)


def onehot(mask):
    return jnp.where(mask, 1.0, 0.0).astype(BF)


def prep_body(rows_ref, lens_ref, counts_ref, out_ref):
    most, pool, slots = rows_ref.shape
    used = iota((most, slots), 0) < counts_ref[...]
    lens = lens_ref[...]
    parts = [
        jnp.where(used & (p < lens), rows_ref[:, p, :], -1) for p in range(pool)
    ]
    wide = jnp.concatenate(parts, axis=0)
    for at in range(slots // 128):
        out_ref[pl.ds(at * 128, 128), :] = wide[:, at * 128 : (at + 1) * 128].T


def prep_ids(rows_ref, lens_ref, counts_ref, ids_out):
    most, pool, slots = rows_ref.shape
    used = iota((most, slots), 0) < counts_ref[...]
    lens = lens_ref[...]
    wide = jnp.concatenate(
        [jnp.where(used & (p < lens), rows_ref[:, p, :], -1) for p in range(pool)], axis=0
    )
    for at in range(slots // 128):
        turned = wide[:, at * 128 : (at + 1) * 128].T.reshape(32, 4, 128)
        ids_out[at * 32 : at * 32 + 32] = turned.astype(jnp.int16)


PLANE = 512


def pool_turn(tables_ref, turned_ref):
    tabs, vocab, width = tables_ref.shape
    for j in range(tabs):
        for at in range(vocab // 128):
            turned_ref[j, at] = (
                tables_ref[j, at * 128 : at * 128 + 128, :].astype(F32).T * (0.25 ** (at % 4))
            ).astype(BF)


def pool_setup(load_ids, y_ref, code_ref, pos_ref, scale_ref):
    lane = iota((32, 128), 1)
    chunk = lane // 32
    same = onehot(iota((128, 128), 0) // 32 == iota((128, 128), 1) // 32)
    base = jnp.zeros((32, 128), F32)
    for j in range(4):
        got = [load_ids(q, j) for q in range(4)]
        ys = []
        for p in range(4):
            y = got[0] if p == 0 else pltpu.roll(got[0], (-p * 32) % 128, 1)
            for q in range(1, 4):
                moved = got[q] if p == q else pltpu.roll(got[q], ((q - p) * 32) % 128, 1)
                y = jnp.where(chunk == q, moved, y)
            ys.append(y)
        valid = ys[0] >= 0
        total = jnp.dot(onehot(valid), same, preferred_element_type=F32)
        place = base.astype(I32) + (lane % 32) + chunk * ROOM
        pos_ref[pl.ds(j * 32, 32), :] = jnp.where(valid, place, -1)
        base = base + total
        alike = (ys[0] == ys[1]) & (ys[0] == ys[2]) & (ys[0] == ys[3])
        scale_ref[pl.ds(j * 32, 32), :] = jnp.where(alike, 2.0, 1.0)
        for p in range(4):
            y = ys[p]
            live = (y >= 0) if p < 2 else ((y >= 0) & ~alike)
            code = jnp.where(live, jnp.left_shift(jnp.ones_like(y), ((y >> 7) * 2) & 31), 0)
            y_ref[pl.ds((j * 4 + p) * 32, 32), :] = y & 127
            for k in range(4):
                code_ref[pl.ds(k * PLANE + (j * 4 + p) * 32, 32), :] = (
                    lax.shift_right_logical(code, jnp.full_like(code, 8 * k)) & 255
                )


def small(ref, at):
    return jnp.broadcast_to(ref[pl.ds(at, 1), :], (16, 128)).astype(jnp.int16)


def pool_table(t, j, turned_ref, y_ref, code_ref, scale_ref, xt_ref):
    low_iota = iota((16, 128), 0).astype(jnp.int16)
    zero = jnp.zeros((16, 128), jnp.int16)
    rows = [[(j * 4 + p) * 32 + 2 * t + half for p in range(4)] for half in range(2)]
    hits = []
    for half in range(2):
        lows = [small(y_ref, row) for row in rows[half]]
        hits.append([[low == low_iota + jnp.int16(16 * at) for low in lows] for at in range(8)])
    total = None
    for k in range(4):
        planes = []
        for half in range(2):
            codes = [small(code_ref, k * PLANE + row) for row in rows[half]]
            plane = []
            for hit in hits[half]:
                cut = [jnp.where(hit[p], codes[p], zero) for p in range(4)]
                plane.append((cut[0] + cut[1]) + (cut[2] + cut[3]))
            planes.append(jnp.concatenate(plane, axis=0).astype(jnp.uint8))
        for i in (0, 2):
            hot = jnp.concatenate(
                [
                    jnp.concatenate([(plane & jnp.uint8(3 << (2 * u))).astype(BF) for u in (i, i + 1)], axis=0)
                    for plane in planes
                ],
                axis=1,
            )
            left = jnp.concatenate([turned_ref[j, 4 * k + i], turned_ref[j, 4 * k + i + 1]], axis=1)
            part = jnp.dot(left, hot, preferred_element_type=F32)
            total = part if total is None else total + part
    for half in range(2):
        scale = scale_ref[pl.ds(j * 32 + 2 * t + half, 1), :]
        xt_ref[half, j] = (total[:, half * 128 : half * 128 + 128] * scale).astype(BF)


def pool_pack(t, pos_ref, xt_ref):
    out = []
    for half in range(2):
        total = None
        for jj in range(2):
            packs, cols = [], []
            for j in (2 * jj, 2 * jj + 1):
                pos = small(pos_ref, j * 32 + 2 * t + half)
                hits = [
                    jnp.where(
                        pos == iota((16, 128), 0).astype(jnp.int16) + jnp.int16(16 * at),
                        jnp.ones((16, 128), BF),
                        jnp.zeros((16, 128), BF),
                    )
                    for at in range(4 * ROOM // 16)
                ]
                packs.append(jnp.concatenate(hits, axis=0))
                cols.append(xt_ref[half, j])
            part = lax.dot_general(
                jnp.concatenate(packs, axis=1),
                jnp.concatenate(cols, axis=1),
                (((1,), (1,)), ((), ())),
                preferred_element_type=F32,
            )
            total = part if total is None else total + part
        out.append(total.astype(BF))
    return out


def pool_step(t, turned_ref, y_ref, code_ref, pos_ref, scale_ref, xt_ref):
    for j in range(4):
        pool_table(t, j, turned_ref, y_ref, code_ref, scale_ref, xt_ref)
    return pool_pack(t, pos_ref, xt_ref)


def pool_body(tables_ref, ids_ref, out_ref, turned_ref, y_ref, code_ref, pos_ref, scale_ref, xt_ref):
    pool_turn(tables_ref, turned_ref)
    pool_setup(
        lambda q, j: ids_ref[pl.ds(q, 32, stride=4), j, :], y_ref, code_ref, pos_ref, scale_ref
    )

    def step(t, carry):
        blocks = pool_step(t, turned_ref, y_ref, code_ref, pos_ref, scale_ref, xt_ref)
        for half in range(2):
            out_ref[pl.ds(pl.multiple_of((2 * t + half) * 4 * ROOM, 4 * ROOM), 4 * ROOM), :] = blocks[half]
        return carry

    lax.fori_loop(0, 16, step, 0)


def pool_scratch():
    return [
        pltpu.VMEM((4, 16, 128, 128), BF),
        pltpu.VMEM((PLANE, 128), I32),
        pltpu.VMEM((4 * PLANE, 128), I32),
        pltpu.VMEM((128, 128), I32),
        pltpu.VMEM((128, 128), F32),
        pltpu.VMEM((2, 4, 128, 128), BF),
    ]


def order_columns(order_ref):
    slots = order_ref.shape[1]
    return onehot(iota((slots, slots), 0) == order_ref[...])


def weight_body(order_ref, top_ref, out_ref, raw_ref, plane_ref, perm_ref, sems):
    slots = out_ref.shape[2]
    copies = [
        pltpu.make_async_copy(top_ref.at[:, pl.ds(at * 128, 128)], raw_ref.at[at], sems.at[at]) for at in range(4)
    ]
    for copy in copies:
        copy.start()
    perm_ref[...] = order_columns(order_ref).astype(F32).T.astype(BF)
    for copy in copies:
        copy.wait()
    weight_cut(raw_ref, plane_ref)
    weight_turn(perm_ref, plane_ref, out_ref)


def weight_cut(raw_ref, plane_ref):
    row = iota((256, 256), 0)
    col = iota((256, 256), 1)
    spread = onehot((col % 16 == row // 16) & (col // 16 == row % 16))

    def cut(i, carry):
        for u in range(4):
            at = i * 4 + u
            rows = pl.ds(pl.multiple_of(at * 256, 256), 256)
            block = jnp.dot(
                spread, jnp.concatenate([raw_ref[c, rows, :] for c in range(4)], axis=1), preferred_element_type=F32
            ).astype(BF)
            for k in range(16):
                for c in range(4):
                    plane_ref[k, c, pl.ds(pl.multiple_of(at * 16, 16), 16), :] = block[
                        k * 16 : k * 16 + 16, c * 128 : c * 128 + 128
                    ]
        return carry

    lax.fori_loop(0, raw_ref.shape[1] // 1024, cut, 0)


def weight_turn(perm_ref, plane_ref, out_ref):
    perm = perm_ref[...]

    def turn(k, carry):
        plane = jnp.concatenate([plane_ref[k, c] for c in range(4)], axis=1)
        done = jnp.dot(perm, plane, preferred_element_type=F32).astype(BF)
        for c in range(4):
            out_ref[k, c] = done[:, c * 128 : c * 128 + 128]
        return carry

    lax.fori_loop(0, 16, turn, 0)


def weight_plane(k, perm_ref, plane_ref, raw_ref):
    plane = jnp.concatenate([plane_ref[k, c] for c in range(4)], axis=1)
    done = jnp.dot(perm_ref[...], plane, preferred_element_type=F32).astype(BF)
    for c in range(4):
        raw_ref[c, pl.ds(pl.multiple_of(k * 512, 512), 512), :] = done[:, c * 128 : c * 128 + 128]


def target_setup(inverse_ref, counts_ref, order_ref, compress_ref, turn_ref, mix_ref):
    samples, slots = inverse_ref.shape
    columns = order_columns(order_ref)
    mix_ref[...] = jnp.dot(compress_ref[...], columns, preferred_element_type=F32).astype(BF)
    chosen = jnp.dot(inverse_ref[...].astype(F32).astype(BF), columns, preferred_element_type=F32)
    counts = jnp.broadcast_to(counts_ref[...], (16, slots)).astype(F32)
    before = (iota((slots, slots), 0) // 4 == iota((slots, slots), 1) // 4) & (
        iota((slots, slots), 0) < iota((slots, slots), 1)
    )
    base = jnp.dot(counts.astype(BF), onehot(before), preferred_element_type=F32)[:1, :]
    offset = ((iota((1, slots), 1) // 4) % 2 * ROOM).astype(F32)
    place = jnp.where(chosen < counts[:1, :], chosen + (base + offset), 255.0)
    for at in range(slots // 128):
        turned = place[:, at * 128 : (at + 1) * 128].T.astype(I32).reshape(8, 16, 128)
        upper, lower = turned[:, :8].reshape(64, 128), turned[:, 8:].reshape(64, 128)
        two = upper | (lower << 8)
        turn_ref[pl.ds(at * 64, 64), :] = two | (pltpu.roll(two, 64, 1) << 16)


def pick_chunk(c, packed_ref, turn_ref, feat_ref):
    place = turn_ref[pl.ds(pl.multiple_of(c * 8, 8), 8), :]
    near = iota((16, 128), 1).astype(jnp.int16)
    far = near + jnp.int16(128)
    one, zero = jnp.ones((16, 128), BF), jnp.zeros((16, 128), BF)
    rows = jnp.concatenate(
        [packed_ref[pl.ds(pl.multiple_of(c * 320 + h * 160, 160), 160), :] for h in range(2)], axis=1
    )
    at = pl.ds(pl.multiple_of(c * 16, 16), 16)
    for part in range(4):
        left, right = [[], []], [[], []]
        for b in range(part * 16, part * 16 + 16):
            x = jnp.broadcast_to(place[:, b : b + 1], (8, 128))
            for v in range(2):
                cut = [(x >> (16 * v)) & 255, (x >> (16 * v + 8)) & 255]
                want = jnp.concatenate(cut, axis=0).astype(jnp.int16)
                left[v].append(jnp.where(want == near, one, zero))
                right[v].append(jnp.where(want == far, one, zero)[:, :32])
        got = jnp.dot(
            jnp.concatenate(
                [jnp.concatenate(left[0] + left[1], axis=0), jnp.concatenate(right[0] + right[1], axis=0)], axis=1
            ),
            rows,
            preferred_element_type=F32,
        ).reshape(2, 16, 16, 256)
        both = jnp.concatenate([got[:, :, :8, :128], got[:, :, 8:, 128:]], axis=2).astype(BF)
        for v in range(2):
            feat_ref[part * 16 : part * 16 + 16, v, at, :] = both[v]


def finish(feat_ref, mix_ref, weight_at, bias_ref, out_ref, left_ref, pair_ref, acc_ref):
    mix = mix_ref[...]
    zero = jnp.zeros((16, 128), BF)

    def mixing(i, carry):
        for u in range(8):
            feats = jnp.concatenate([feat_ref[i * 8 + u, v] for v in range(2)], axis=1)
            mixed = jnp.dot(mix, feats, preferred_element_type=F32).astype(BF)
            for v in range(2):
                left_ref[i * 8 + u, v, v * 16 : v * 16 + 16, :] = mixed[:, v * 128 : v * 128 + 128]
                left_ref[i * 8 + u, v, 16 - v * 16 : 32 - v * 16, :] = zero
        return carry

    lax.fori_loop(0, 8, mixing, 0)

    def pairing(i, carry):
        for u in range(8):
            sides = [
                jnp.concatenate([ref[i * 8 + u, v] for v in range(2)], axis=1) for ref in (left_ref, feat_ref)
            ]
            both = lax.dot_general(
                sides[0], sides[1], (((1,), (1,)), ((), ())), preferred_element_type=F32
            )
            for v in range(2):
                to = pl.ds(pl.multiple_of((v * 64 + i * 8 + u) * 24, 8), 16)
                for at in range(4):
                    pair_ref[at, to, :] = both[v * 16 : v * 16 + 16, at * 128 : at * 128 + 128]
        return carry

    lax.fori_loop(0, 8, pairing, 0)
    acc_ref[...] = jnp.broadcast_to(bias_ref[...], acc_ref.shape)

    def plane(i, carry):
        total = acc_ref[...]
        for u in range(4):
            k = i * 4 + u
            lhs = jnp.concatenate(
                [pair_ref[at, pl.ds(k, 128, stride=24), :].astype(BF) for at in range(4)], axis=1
            )
            total = total + jnp.dot(
                lhs, jnp.concatenate([weight_at(k, at) for at in range(4)], axis=1), preferred_element_type=F32)
        acc_ref[...] = total
        return carry

    lax.fori_loop(0, 4, plane, 0)
    out_ref[...] = jnp.maximum(acc_ref[...], 0.0).astype(BF)


def score_body(
    packed_ref, inverse_ref, counts_ref, order_ref, compress_ref, weight_ref, bias_ref,
    out_ref, turn_ref, mix_ref, feat_ref, left_ref, pair_ref, acc_ref,
):
    target_setup(inverse_ref, counts_ref, order_ref, compress_ref, turn_ref, mix_ref)

    def chunk(c, carry):
        pick_chunk(c, packed_ref, turn_ref, feat_ref)
        return carry

    lax.fori_loop(0, 32, chunk, 0)
    finish(feat_ref, mix_ref, lambda k, at: weight_ref[k, at], bias_ref, out_ref, left_ref, pair_ref, acc_ref)


def score_scratch():
    return [
        pltpu.VMEM((256, 128), I32),
        pltpu.VMEM((16, 512), BF),
        pltpu.VMEM((64, 2, 512, 128), BF),
        pltpu.VMEM((64, 2, 32, 128), BF),
        pltpu.VMEM((4, 3072, 128), F32),
        pltpu.VMEM((128, 512), F32),
    ]


VM = pl.BlockSpec(memory_space=pltpu.VMEM)
BIG = 60 * 1024 * 1024


def call(body, outs, scratch, count, flops, **kw):
    return pl.pallas_call(
        body,
        out_shape=outs,
        in_specs=[VM] * count,
        out_specs=VM,
        scratch_shapes=scratch,
        compiler_params=pltpu.CompilerParams(vmem_limit_bytes=BIG, **kw),
        cost_estimate=pl.CostEstimate(flops=flops, bytes_accessed=4 << 20, transcendentals=0),
    )


def weight_call(order, top):
    slots, units = order.shape[1], top.shape[1]
    shape = (16, units // 128, slots, 128)
    return pl.pallas_call(
        weight_body,
        out_shape=jax.ShapeDtypeStruct(shape, BF),
        in_specs=[VM, pl.BlockSpec(memory_space=pl.ANY)],
        out_specs=VM,
        scratch_shapes=[
            pltpu.VMEM((units // 128, top.shape[0], 128), BF),
            pltpu.VMEM(shape, BF),
            pltpu.VMEM((slots, slots), BF),
            pltpu.SemaphoreType.DMA((4,)),
        ],
        compiler_params=pltpu.CompilerParams(vmem_limit_bytes=BIG),
        cost_estimate=pl.CostEstimate(flops=6 * 10**9, bytes_accessed=16 << 20, transcendentals=0),
    )(order, top)


MESH = pl.DeviceIdType.MESH
GROUPS = 16


def lookup_body(
    rows_ref, lens_ref, counts_ref, inverse_ref, order_ref, compress_ref, bias_ref, tables_hbm, top_hbm,
    out_ref,
    tables_ref, turned_ref, y_ref, code_ref, pos_ref, scale_ref, xt_ref,
    raw_ref, plane_ref, perm_ref, ids_out, ids_in, ids_wide, send_ref, recv_ref,
    turn_ref, mix_ref, feat_ref, left_ref, pair_ref, acc_ref,
    local_sems, ids_sems, send_sem, recv_sems,
):
    n = 8 * GROUPS
    me = lax.axis_index("dev")
    my_group, my_place = me // 8, me % 8
    my_z, my_y = my_group // 2, my_group % 2

    barrier = pltpu.get_barrier_semaphore()

    def greet(i, carry):
        pl.semaphore_signal(barrier, 1, device_id={"dev": (me + i) % n}, device_id_type=MESH)
        return carry

    lax.fori_loop(1, n, greet, 0)
    copies = [pltpu.make_async_copy(tables_hbm, tables_ref, local_sems.at[4])] + [
        pltpu.make_async_copy(top_hbm.at[:, pl.ds(at * 128, 128)], raw_ref.at[at], local_sems.at[at])
        for at in range(4)
    ]
    for copy in copies:
        copy.start()

    prep_ids(rows_ref, lens_ref, counts_ref, ids_out)
    ids_in[me] = ids_out[me]
    pl.semaphore_wait(barrier, n - 1)

    def id_copy(src, dst, to):
        return pltpu.make_async_remote_copy(
            src_ref=src, dst_ref=dst, send_sem=ids_sems.at[0], recv_sem=ids_sems.at[1],
            device_id={"dev": to}, device_id_type=MESH,
        )

    def send_ids(i, carry):
        to = (me + i) % n
        id_copy(ids_out.at[to], ids_in.at[me], to).start()
        return carry

    lax.fori_loop(1, n, send_ids, 0)

    copies[0].wait()
    pool_turn(tables_ref, turned_ref)
    target_setup(inverse_ref, counts_ref, order_ref, compress_ref, turn_ref, mix_ref)
    perm_ref[...] = order_columns(order_ref).astype(F32).T.astype(BF)
    for copy in copies[1:]:
        copy.wait()
    weight_cut(raw_ref, plane_ref)

    everyone = id_copy(ids_out.at[pl.ds(0, n - 1)], ids_in.at[pl.ds(0, n - 1)], (me + 1) % n)
    everyone.wait_recv()
    ids_wide[...] = ids_in[...].astype(I32)
    pool_setup(
        lambda q, j: ids_wide[pl.ds(q, 32, stride=4), j, :], y_ref, code_ref, pos_ref, scale_ref
    )

    def shift(t):
        m = t // 2
        return 4 + ((m + 1) // 2) * (1 - 2 * (m % 2))

    def row_copy(src, dst, to, group):
        return pltpu.make_async_remote_copy(
            src_ref=src, dst_ref=dst, send_sem=send_sem.at[0], recv_sem=recv_sems.at[group],
            device_id={"dev": to}, device_id_type=MESH,
        )

    def block(ref, device):
        return ref.at[pl.ds(pl.multiple_of(device * ROOM, ROOM), ROOM), :]

    def target(t):
        return 2 * ((my_z + shift(t)) % 8) + (my_y + t) % 2

    def send_group(t):
        group = target(t)

        def one(i, carry):
            to = group * 8 + (my_place + i) % 8

            @pl.when(to != me)
            def _():
                row_copy(block(send_ref, to), block(recv_ref, me), to, my_group).start()

            return carry

        lax.fori_loop(0, 8, one, 0)

    def step(t, carry):
        group = target(t)
        pool_table(group, 0, turned_ref, y_ref, code_ref, scale_ref, xt_ref)

        @pl.when(t > 0)
        def _():
            send_group(t - 1)

        for j in range(1, 4):
            pool_table(group, j, turned_ref, y_ref, code_ref, scale_ref, xt_ref)
        blocks = pool_pack(group, pos_ref, xt_ref)
        for half in range(2):
            send_ref[pl.ds(pl.multiple_of((2 * group + half) * 4 * ROOM, 4 * ROOM), 4 * ROOM), :] = blocks[half]
        weight_plane(t, perm_ref, plane_ref, raw_ref)
        return carry

    lax.fori_loop(0, GROUPS, step, 0)
    send_group(GROUPS - 1)
    mine = pl.ds(pl.multiple_of(me * ROOM, ROOM), ROOM)
    recv_ref[mine, :] = send_ref[mine, :]

    def arrive(u, carry):
        group = 2 * ((my_z + 8 - shift(u)) % 8) + (my_y + u) % 2

        @pl.when(group == my_group)
        def _():
            rows = pl.ds(0, 7 * ROOM)
            row_copy(send_ref.at[rows, :], recv_ref.at[rows, :], (me + 1) % n, group).wait_recv()

        @pl.when(group != my_group)
        def _():
            rows = pl.ds(0, 8 * ROOM)
            row_copy(send_ref.at[rows, :], recv_ref.at[rows, :], (me + 1) % n, group).wait_recv()

        for v in range(2):
            pick_chunk(2 * group + v, recv_ref, turn_ref, feat_ref)
        return carry

    lax.fori_loop(0, GROUPS, arrive, 0)
    finish(
        feat_ref, mix_ref, lambda k, at: raw_ref[at, pl.ds(pl.multiple_of(k * 512, 512), 512), :],
        bias_ref, out_ref, left_ref, pair_ref, acc_ref,
    )
    everyone.wait_send()
    rows = pl.ds(0, (n - 1) * ROOM)
    row_copy(send_ref.at[rows, :], recv_ref.at[rows, :], (me + 1) % n, my_group).wait_send()


def shards(tables, bag_rows, bag_lengths, row_counts, inverse, table_order, compress, top_weight, top_bias):
    order = table_order.reshape(1, -1)
    bias = top_bias.reshape(1, -1)
    rows = bag_rows[0].transpose(1, 2, 0)
    lens = bag_lengths[0].transpose(1, 0)
    samples, units = inverse.shape[0], top_weight.shape[1]
    anywhere = pl.BlockSpec(memory_space=pl.ANY)
    scratch = (
        [pltpu.VMEM(tables.shape, BF)]
        + pool_scratch()
        + [
            pltpu.VMEM((units // 128, top_weight.shape[0], 128), BF),
            pltpu.VMEM((16, units // 128, 512, 128), BF),
            pltpu.VMEM((512, 512), BF),
            pltpu.VMEM((128, 4, 128), jnp.int16),
            pltpu.VMEM((128, 4, 128), jnp.int16),
            pltpu.VMEM((128, 4, 128), I32),
            pltpu.VMEM((128 * ROOM, 128), BF),
            pltpu.VMEM((128 * ROOM, 128), BF),
        ]
        + score_scratch()
        + [
            pltpu.SemaphoreType.DMA((5,)),
            pltpu.SemaphoreType.DMA((2,)),
            pltpu.SemaphoreType.DMA((1,)),
            pltpu.SemaphoreType.DMA((GROUPS,)),
        ]
    )
    return pl.pallas_call(
        lookup_body,
        out_shape=jax.ShapeDtypeStruct((samples, units), BF),
        in_specs=[VM] * 7 + [anywhere] * 2,
        out_specs=VM,
        scratch_shapes=scratch,
        compiler_params=pltpu.CompilerParams(vmem_limit_bytes=BIG, collective_id=0, has_side_effects=True),
        cost_estimate=pl.CostEstimate(flops=3 * 10**10, bytes_accessed=16 << 20, transcendentals=0),
    )(rows, lens, row_counts, inverse, order, compress, bias, tables, top_weight)


def solution(mesh):
    return jax.shard_map(
        shards,
        mesh=mesh,
        in_specs=(
            P("dev", None, None),
            P(("rep", "dev"), None, None, None),
            P(("rep", "dev"), None, None),
            P(("rep", "dev"), None),
            P(("rep", "dev"), None),
            P(),
            P(),
            P(),
            P(),
        ),
        out_specs=P(("rep", "dev"), None),
        check_vma=False,
    )
```

time: 208 us -> 104 us (0.50)
  waiting for transfers between devices: 40.7 us -> 0 us
  blocking collectives: 30.1 us -> 0 us
  Pallas kernels: 129 us -> 101 us
  starting transfers between devices: 6.64 us -> 0 us
    all_to_all x1 -> x0, waiting for transfers between devices: 40.7 us -> none  [shards(): lax.all_to_all(packed.reshape(128, ROOM, 128), 'dev', split_axis=0, conca...]
    all_to_all x1 -> x0, blocking collectives: 30.1 us -> none  [shards(): lax.all_to_all(ids.reshape(128, 4, 128), 'dev', split_axis=0, concat_axis...]
    pallas_call x4 -> x1, Pallas kernels: 129 us -> 101 us  [shards(): pl.pallas_call(lookup_body, out_shape=jax.ShapeDtypeStruct((samples, unit...]
    all_to_all x1 -> x0, starting transfers between devices: 6.64 us -> none  [shards(): lax.all_to_all(packed.reshape(128, ROOM, 128), 'dev', split_axis=0, conca...]
  transfers between devices with their start and end apart: 1 -> 0, of which waited for: 1 -> 0; matrix products, arithmetic and copies ran while one was open for 0% -> 0% of each run, Pallas kernels for 10% -> 0%
where the time goes in v2:
time: 104 us; the launch traced here: 102 us
  Pallas kernels  101 us (97%)
  local copies, waits for them, and re-layouts  1.57 us (2%)
    pallas_call x1, Pallas kernels, shards(): pl.pallas_call(lookup_body, out_shape=jax.ShapeDtypeStruct((samples, unit...  101 us

profile of v2, /device:TPU:8, one launch (start us, length us, event | category | flops | bytes accessed | tf_op | source)
XLA Modules:
  0.0 102.1 jit_solution(3631461169147181102)
XLA Ops:
  0.0 100.6 %shard_map.91 = bf16[128,512]{1,0:T(8,128)(2,1)} custom-call(s32[32,4,512]{2,1,0:T(4,128)} %bitcast.8, s32[32,512]{1,0:T(8,128)} %bitcast.9, s32[1,512]{1,0:T(1,128)} %counts_ref.1, s32[128,512]{1,0:T(8,128)} %inverse_ref.1, s32[1,512]{1,0:T(1,128)} %bitcast.10, bf16[16,512]{1,0:T(8,128)(2,1)} %compress_ref.1, f32[1,512]{1,0:T(1,128)} %bitcast.11, ...), custom_call_target="tpu_custom_call" | custom-call | flops 30000001024 | bytes 16777216 | tf_op jit(solution)/shard_map/pallas_call | solution.py:577
  100.6 1.6 %copy.11 = bf16[128,512]{1,0:T(8,128)(2,1)} copy(bf16[128,512]{1,0:T(8,128)(2,1)} %shard_map.91) | data formatting | bytes 262144

commit v3 on v2

--- a/solution.py
+++ b/solution.py
@@ -18,18 +18,6 @@
 
 def onehot(mask):
     return jnp.where(mask, 1.0, 0.0).astype(BF)
-
-
-def prep_body(rows_ref, lens_ref, counts_ref, out_ref):
-    most, pool, slots = rows_ref.shape
-    used = iota((most, slots), 0) < counts_ref[...]
-    lens = lens_ref[...]
-    parts = [
-        jnp.where(used & (p < lens), rows_ref[:, p, :], -1) for p in range(pool)
-    ]
-    wide = jnp.concatenate(parts, axis=0)
-    for at in range(slots // 128):
-        out_ref[pl.ds(at * 128, 128), :] = wide[:, at * 128 : (at + 1) * 128].T
 
 
 def prep_ids(rows_ref, lens_ref, counts_ref, ids_out):
@@ -161,21 +149,6 @@
     return pool_pack(t, pos_ref, xt_ref)
 
 
-def pool_body(tables_ref, ids_ref, out_ref, turned_ref, y_ref, code_ref, pos_ref, scale_ref, xt_ref):
-    pool_turn(tables_ref, turned_ref)
-    pool_setup(
-        lambda q, j: ids_ref[pl.ds(q, 32, stride=4), j, :], y_ref, code_ref, pos_ref, scale_ref
-    )
-
-    def step(t, carry):
-        blocks = pool_step(t, turned_ref, y_ref, code_ref, pos_ref, scale_ref, xt_ref)
-        for half in range(2):
-            out_ref[pl.ds(pl.multiple_of((2 * t + half) * 4 * ROOM, 4 * ROOM), 4 * ROOM), :] = blocks[half]
-        return carry
-
-    lax.fori_loop(0, 16, step, 0)
-
-
 def pool_scratch():
     return [
         pltpu.VMEM((4, 16, 128, 128), BF),
@@ -192,53 +165,19 @@
     return onehot(iota((slots, slots), 0) == order_ref[...])
 
 
-def weight_body(order_ref, top_ref, out_ref, raw_ref, plane_ref, perm_ref, sems):
-    slots = out_ref.shape[2]
-    copies = [
-        pltpu.make_async_copy(top_ref.at[:, pl.ds(at * 128, 128)], raw_ref.at[at], sems.at[at]) for at in range(4)
-    ]
-    for copy in copies:
-        copy.start()
-    perm_ref[...] = order_columns(order_ref).astype(F32).T.astype(BF)
-    for copy in copies:
-        copy.wait()
-    weight_cut(raw_ref, plane_ref)
-    weight_turn(perm_ref, plane_ref, out_ref)
-
-
-def weight_cut(raw_ref, plane_ref):
+def weight_cut(at, raw_ref, plane_ref):
     row = iota((256, 256), 0)
     col = iota((256, 256), 1)
     spread = onehot((col % 16 == row // 16) & (col // 16 == row % 16))
-
-    def cut(i, carry):
-        for u in range(4):
-            at = i * 4 + u
-            rows = pl.ds(pl.multiple_of(at * 256, 256), 256)
-            block = jnp.dot(
-                spread, jnp.concatenate([raw_ref[c, rows, :] for c in range(4)], axis=1), preferred_element_type=F32
-            ).astype(BF)
-            for k in range(16):
-                for c in range(4):
-                    plane_ref[k, c, pl.ds(pl.multiple_of(at * 16, 16), 16), :] = block[
-                        k * 16 : k * 16 + 16, c * 128 : c * 128 + 128
-                    ]
-        return carry
-
-    lax.fori_loop(0, raw_ref.shape[1] // 1024, cut, 0)
-
-
-def weight_turn(perm_ref, plane_ref, out_ref):
-    perm = perm_ref[...]
-
-    def turn(k, carry):
-        plane = jnp.concatenate([plane_ref[k, c] for c in range(4)], axis=1)
-        done = jnp.dot(perm, plane, preferred_element_type=F32).astype(BF)
+    rows = pl.ds(pl.multiple_of(at * 256, 256), 256)
+    block = jnp.dot(
+        spread, jnp.concatenate([raw_ref[c, rows, :] for c in range(4)], axis=1), preferred_element_type=F32
+    ).astype(BF)
+    for k in range(16):
         for c in range(4):
-            out_ref[k, c] = done[:, c * 128 : c * 128 + 128]
-        return carry
-
-    lax.fori_loop(0, 16, turn, 0)
+            plane_ref[k, c, pl.ds(pl.multiple_of(at * 16, 16), 16), :] = block[
+                k * 16 : k * 16 + 16, c * 128 : c * 128 + 128
+            ]
 
 
 def weight_plane(k, perm_ref, plane_ref, raw_ref):
@@ -297,21 +236,17 @@
             feat_ref[part * 16 : part * 16 + 16, v, at, :] = both[v]
 
 
-def finish(feat_ref, mix_ref, weight_at, bias_ref, out_ref, left_ref, pair_ref, acc_ref):
-    mix = mix_ref[...]
-    zero = jnp.zeros((16, 128), BF)
-
-    def mixing(i, carry):
+def mixing(columns, feats_of, store):
+    def some(i, carry):
         for u in range(8):
-            feats = jnp.concatenate([feat_ref[i * 8 + u, v] for v in range(2)], axis=1)
-            mixed = jnp.dot(mix, feats, preferred_element_type=F32).astype(BF)
-            for v in range(2):
-                left_ref[i * 8 + u, v, v * 16 : v * 16 + 16, :] = mixed[:, v * 128 : v * 128 + 128]
-                left_ref[i * 8 + u, v, 16 - v * 16 : 32 - v * 16, :] = zero
+            feats = jnp.concatenate([feats_of(i * 8 + u, v) for v in range(2)], axis=1)
+            store(i * 8 + u, jnp.dot(columns, feats, preferred_element_type=F32))
         return carry
 
-    lax.fori_loop(0, 8, mixing, 0)
-
+    lax.fori_loop(0, 8, some, 0)
+
+
+def finish(feat_ref, weight_at, bias_ref, out_ref, left_ref, pair_ref, acc_ref):
     def pairing(i, carry):
         for u in range(8):
             sides = [
@@ -345,26 +280,13 @@
     out_ref[...] = jnp.maximum(acc_ref[...], 0.0).astype(BF)
 
 
-def score_body(
-    packed_ref, inverse_ref, counts_ref, order_ref, compress_ref, weight_ref, bias_ref,
-    out_ref, turn_ref, mix_ref, feat_ref, left_ref, pair_ref, acc_ref,
-):
-    target_setup(inverse_ref, counts_ref, order_ref, compress_ref, turn_ref, mix_ref)
-
-    def chunk(c, carry):
-        pick_chunk(c, packed_ref, turn_ref, feat_ref)
-        return carry
-
-    lax.fori_loop(0, 32, chunk, 0)
-    finish(feat_ref, mix_ref, lambda k, at: weight_ref[k, at], bias_ref, out_ref, left_ref, pair_ref, acc_ref)
-
-
 def score_scratch():
     return [
         pltpu.VMEM((256, 128), I32),
         pltpu.VMEM((16, 512), BF),
         pltpu.VMEM((64, 2, 512, 128), BF),
         pltpu.VMEM((64, 2, 32, 128), BF),
+        pltpu.VMEM((64, 16, 256), F32),
         pltpu.VMEM((4, 3072, 128), F32),
         pltpu.VMEM((128, 512), F32),
     ]
@@ -372,37 +294,6 @@
 
 VM = pl.BlockSpec(memory_space=pltpu.VMEM)
 BIG = 60 * 1024 * 1024
-
-
-def call(body, outs, scratch, count, flops, **kw):
-    return pl.pallas_call(
-        body,
-        out_shape=outs,
-        in_specs=[VM] * count,
-        out_specs=VM,
-        scratch_shapes=scratch,
-        compiler_params=pltpu.CompilerParams(vmem_limit_bytes=BIG, **kw),
-        cost_estimate=pl.CostEstimate(flops=flops, bytes_accessed=4 << 20, transcendentals=0),
-    )
-
-
-def weight_call(order, top):
-    slots, units = order.shape[1], top.shape[1]
-    shape = (16, units // 128, slots, 128)
-    return pl.pallas_call(
-        weight_body,
-        out_shape=jax.ShapeDtypeStruct(shape, BF),
-        in_specs=[VM, pl.BlockSpec(memory_space=pl.ANY)],
-        out_specs=VM,
-        scratch_shapes=[
-            pltpu.VMEM((units // 128, top.shape[0], 128), BF),
-            pltpu.VMEM(shape, BF),
-            pltpu.VMEM((slots, slots), BF),
-            pltpu.SemaphoreType.DMA((4,)),
-        ],
-        compiler_params=pltpu.CompilerParams(vmem_limit_bytes=BIG),
-        cost_estimate=pl.CostEstimate(flops=6 * 10**9, bytes_accessed=16 << 20, transcendentals=0),
-    )(order, top)
 
 
 MESH = pl.DeviceIdType.MESH
@@ -414,21 +305,40 @@
     out_ref,
     tables_ref, turned_ref, y_ref, code_ref, pos_ref, scale_ref, xt_ref,
     raw_ref, plane_ref, perm_ref, ids_out, ids_in, ids_wide, send_ref, recv_ref,
-    turn_ref, mix_ref, feat_ref, left_ref, pair_ref, acc_ref,
+    turn_ref, mix_ref, feat_ref, left_ref, sum_ref, pair_ref, acc_ref, cols_ref,
     local_sems, ids_sems, send_sem, recv_sems,
 ):
     n = 8 * GROUPS
     me = lax.axis_index("dev")
-    my_group, my_place = me // 8, me % 8
+    my_group, my_place, my_chunk = me // 8, me % 8, me // 4
     my_z, my_y = my_group // 2, my_group % 2
 
+    def shift(t):
+        m = t // 2
+        m = m - jnp.where(m > 3, 1, 0)
+        far = 4 + ((m + 1) // 2) * (1 - 2 * (m % 2))
+        return jnp.where(t // 2 == 3, 0, far)
+
+    def target(t):
+        return 2 * ((my_z + shift(t)) % 8) + (my_y + t) % 2
+
+    def each_other(act):
+        def some(t, carry):
+            def one(i, inner):
+                to = target(t) * 8 + (my_place + i) % 8
+
+                @pl.when(to != me)
+                def _():
+                    act(to)
+
+                return inner
+
+            return lax.fori_loop(0, 8, one, carry)
+
+        lax.fori_loop(0, GROUPS, some, 0)
+
     barrier = pltpu.get_barrier_semaphore()
-
-    def greet(i, carry):
-        pl.semaphore_signal(barrier, 1, device_id={"dev": (me + i) % n}, device_id_type=MESH)
-        return carry
-
-    lax.fori_loop(1, n, greet, 0)
+    each_other(lambda to: pl.semaphore_signal(barrier, 1, device_id={"dev": to}, device_id_type=MESH))
     copies = [pltpu.make_async_copy(tables_hbm, tables_ref, local_sems.at[4])] + [
         pltpu.make_async_copy(top_hbm.at[:, pl.ds(at * 128, 128)], raw_ref.at[at], local_sems.at[at])
         for at in range(4)
@@ -438,6 +348,9 @@
 
     prep_ids(rows_ref, lens_ref, counts_ref, ids_out)
     ids_in[me] = ids_out[me]
+    target_setup(inverse_ref, counts_ref, order_ref, compress_ref, turn_ref, mix_ref)
+    copies[0].wait()
+    pool_turn(tables_ref, turned_ref)
     pl.semaphore_wait(barrier, n - 1)
 
     def id_copy(src, dst, to):
@@ -446,20 +359,22 @@
             device_id={"dev": to}, device_id_type=MESH,
         )
 
-    def send_ids(i, carry):
-        to = (me + i) % n
-        id_copy(ids_out.at[to], ids_in.at[me], to).start()
+    each_other(lambda to: id_copy(ids_out.at[to], ids_in.at[me], to).start())
+    perm_ref[...] = order_columns(order_ref).astype(F32).T.astype(BF)
+    for g in range(GROUPS):
+        cols_ref[g] = mix_ref[:, g * 32 : g * 32 + 32]
+
+    def clear(g, carry):
+        rows = pl.ds(pl.multiple_of(arrived(GROUPS - 4 + g) * 32, 32), 32)
+        feat_ref[:, :, rows, :] = jnp.zeros((64, 2, 32, 128), BF)
         return carry
 
-    lax.fori_loop(1, n, send_ids, 0)
-
-    copies[0].wait()
-    pool_turn(tables_ref, turned_ref)
-    target_setup(inverse_ref, counts_ref, order_ref, compress_ref, turn_ref, mix_ref)
-    perm_ref[...] = order_columns(order_ref).astype(F32).T.astype(BF)
+    def arrived(u):
+        return 2 * ((my_z + 8 - shift(u)) % 8) + (my_y + u) % 2
+
+    lax.fori_loop(0, 4, clear, 0)
     for copy in copies[1:]:
         copy.wait()
-    weight_cut(raw_ref, plane_ref)
 
     everyone = id_copy(ids_out.at[pl.ds(0, n - 1)], ids_in.at[pl.ds(0, n - 1)], (me + 1) % n)
     everyone.wait_recv()
@@ -468,82 +383,98 @@
         lambda q, j: ids_wide[pl.ds(q, 32, stride=4), j, :], y_ref, code_ref, pos_ref, scale_ref
     )
 
-    def shift(t):
-        m = t // 2
-        return 4 + ((m + 1) // 2) * (1 - 2 * (m % 2))
-
-    def row_copy(src, dst, to, group):
+    def row_copy(src, dst, to, chunk):
         return pltpu.make_async_remote_copy(
-            src_ref=src, dst_ref=dst, send_sem=send_sem.at[0], recv_sem=recv_sems.at[group],
+            src_ref=src, dst_ref=dst, send_sem=send_sem.at[0], recv_sem=recv_sems.at[chunk],
             device_id={"dev": to}, device_id_type=MESH,
         )
 
     def block(ref, device):
         return ref.at[pl.ds(pl.multiple_of(device * ROOM, ROOM), ROOM), :]
 
-    def target(t):
-        return 2 * ((my_z + shift(t)) % 8) + (my_y + t) % 2
-
-    def send_group(t):
-        group = target(t)
-
-        def one(i, carry):
-            to = group * 8 + (my_place + i) % 8
-
-            @pl.when(to != me)
-            def _():
-                row_copy(block(send_ref, to), block(recv_ref, me), to, my_group).start()
-
-            return carry
-
-        lax.fori_loop(0, 8, one, 0)
-
     def step(t, carry):
         group = target(t)
-        pool_table(group, 0, turned_ref, y_ref, code_ref, scale_ref, xt_ref)
-
-        @pl.when(t > 0)
-        def _():
-            send_group(t - 1)
-
-        for j in range(1, 4):
+        for j in range(4):
             pool_table(group, j, turned_ref, y_ref, code_ref, scale_ref, xt_ref)
         blocks = pool_pack(group, pos_ref, xt_ref)
         for half in range(2):
             send_ref[pl.ds(pl.multiple_of((2 * group + half) * 4 * ROOM, 4 * ROOM), 4 * ROOM), :] = blocks[half]
-        weight_plane(t, perm_ref, plane_ref, raw_ref)
+        for u in range(2):
+            weight_cut(2 * t + u, raw_ref, plane_ref)
+
+        def one(i, inner):
+            to = group * 8 + (my_place + i) % 8
+
+            @pl.when(to != me)
+            def _():
+                row_copy(block(send_ref, to), block(recv_ref, me), to, my_chunk).start()
+
+            return inner
+
+        lax.fori_loop(0, 8, one, 0)
         return carry
 
     lax.fori_loop(0, GROUPS, step, 0)
-    send_group(GROUPS - 1)
     mine = pl.ds(pl.multiple_of(me * ROOM, ROOM), ROOM)
     recv_ref[mine, :] = send_ref[mine, :]
 
-    def arrive(u, carry):
-        group = 2 * ((my_z + 8 - shift(u)) % 8) + (my_y + u) % 2
-
-        @pl.when(group == my_group)
-        def _():
-            rows = pl.ds(0, 7 * ROOM)
-            row_copy(send_ref.at[rows, :], recv_ref.at[rows, :], (me + 1) % n, group).wait_recv()
-
-        @pl.when(group != my_group)
-        def _():
-            rows = pl.ds(0, 8 * ROOM)
-            row_copy(send_ref.at[rows, :], recv_ref.at[rows, :], (me + 1) % n, group).wait_recv()
-
+    def take(u, carry):
+        group = arrived(u)
+
+        def half(v, inner):
+            chunk = 2 * group + (my_chunk + v) % 2
+
+            @pl.when(chunk == my_chunk)
+            def _():
+                rows = pl.ds(0, 3 * ROOM)
+                row_copy(send_ref.at[rows, :], recv_ref.at[rows, :], (me + 1) % n, chunk).wait_recv()
+
+            @pl.when(chunk != my_chunk)
+            def _():
+                rows = pl.ds(0, 4 * ROOM)
+                row_copy(send_ref.at[rows, :], recv_ref.at[rows, :], (me + 1) % n, chunk).wait_recv()
+
+            pick_chunk(chunk, recv_ref, turn_ref, feat_ref)
+            return inner
+
+        return lax.fori_loop(0, 2, half, carry)
+
+    def turn_and_take(u, carry):
+        for k in range(2):
+            weight_plane(2 * u + k, perm_ref, plane_ref, raw_ref)
+        return take(u, carry)
+
+    lax.fori_loop(0, 8, turn_and_take, 0)
+    lax.fori_loop(8, GROUPS - 4, take, 0)
+
+    def keep(i, value):
+        sum_ref[i] = value
+
+    mixing(mix_ref[...], lambda i, v: feat_ref[i, v], keep)
+    lax.fori_loop(GROUPS - 4, GROUPS, take, 0)
+    last = [arrived(GROUPS - 4 + g) for g in range(4)]
+    zero = jnp.zeros((16, 128), BF)
+
+    def settle(i, value):
+        mixed = (sum_ref[i] + value).astype(BF)
         for v in range(2):
-            pick_chunk(2 * group + v, recv_ref, turn_ref, feat_ref)
-        return carry
-
-    lax.fori_loop(0, GROUPS, arrive, 0)
+            left_ref[i, v, v * 16 : v * 16 + 16, :] = mixed[:, v * 128 : v * 128 + 128]
+            left_ref[i, v, 16 - v * 16 : 32 - v * 16, :] = zero
+
+    mixing(
+        jnp.concatenate([cols_ref[g] for g in last], axis=1),
+        lambda i, v: jnp.concatenate(
+            [feat_ref[i, v, pl.ds(pl.multiple_of(g * 32, 32), 32), :] for g in last], axis=0
+        ),
+        settle,
+    )
     finish(
-        feat_ref, mix_ref, lambda k, at: raw_ref[at, pl.ds(pl.multiple_of(k * 512, 512), 512), :],
+        feat_ref, lambda k, at: raw_ref[at, pl.ds(pl.multiple_of(k * 512, 512), 512), :],
         bias_ref, out_ref, left_ref, pair_ref, acc_ref,
     )
     everyone.wait_send()
     rows = pl.ds(0, (n - 1) * ROOM)
-    row_copy(send_ref.at[rows, :], recv_ref.at[rows, :], (me + 1) % n, my_group).wait_send()
+    row_copy(send_ref.at[rows, :], recv_ref.at[rows, :], (me + 1) % n, my_chunk).wait_send()
 
 
 def shards(tables, bag_rows, bag_lengths, row_counts, inverse, table_order, compress, top_weight, top_bias):
@@ -567,11 +498,12 @@
             pltpu.VMEM((128 * ROOM, 128), BF),
         ]
         + score_scratch()
+        + [pltpu.VMEM((GROUPS, 16, 32), BF)]
         + [
             pltpu.SemaphoreType.DMA((5,)),
             pltpu.SemaphoreType.DMA((2,)),
             pltpu.SemaphoreType.DMA((1,)),
-            pltpu.SemaphoreType.DMA((GROUPS,)),
+            pltpu.SemaphoreType.DMA((2 * GROUPS,)),
         ]
     )
     return pl.pallas_call(

time: 104 us -> 104 us (level)
  no operation moved by 1% of the time
where the time goes in v3:
time: 104 us; the launch traced here: 102 us
  Pallas kernels  101 us (97%)
  local copies, waits for them, and re-layouts  1.57 us (2%)
    pallas_call x1, Pallas kernels, shards(): pl.pallas_call(lookup_body, out_shape=jax.ShapeDtypeStruct((samples, unit...  101 us

profile of v3, /device:TPU:8, one launch (start us, length us, event | category | flops | bytes accessed | tf_op | source)
XLA Modules:
  0.0 102.5 jit_solution(17072332592788896058)
XLA Ops:
  0.0 100.9 %shard_map.91 = bf16[128,512]{1,0:T(8,128)(2,1)} custom-call(s32[32,4,512]{2,1,0:T(4,128)} %bitcast.8, s32[32,512]{1,0:T(8,128)} %bitcast.9, s32[1,512]{1,0:T(1,128)} %counts_ref.1, s32[128,512]{1,0:T(8,128)} %inverse_ref.1, s32[1,512]{1,0:T(1,128)} %bitcast.10, bf16[16,512]{1,0:T(8,128)(2,1)} %compress_ref.1, f32[1,512]{1,0:T(1,128)} %bitcast.11, ...), custom_call_target="tpu_custom_call" | custom-call | flops 30000001024 | bytes 16777216 | tf_op jit(solution)/shard_map/pallas_call | solution.py:509
  100.9 1.6 %copy.11 = bf16[128,512]{1,0:T(8,128)(2,1)} copy(bf16[128,512]{1,0:T(8,128)(2,1)} %shard_map.91) | data formatting | bytes 262144

commit v4 on v3

--- a/solution.py
+++ b/solution.py
@@ -277,7 +277,7 @@
         return carry
 
     lax.fori_loop(0, 4, plane, 0)
-    out_ref[...] = jnp.maximum(acc_ref[...], 0.0).astype(BF)
+    out_ref[...] = acc_ref[...]
 
 
 def score_scratch():
@@ -293,7 +293,7 @@
 
 
 VM = pl.BlockSpec(memory_space=pltpu.VMEM)
-BIG = 60 * 1024 * 1024
+BIG = 56 * 1024 * 1024
 
 
 MESH = pl.DeviceIdType.MESH
@@ -324,18 +324,14 @@
 
     def each_other(act):
         def some(t, carry):
-            def one(i, inner):
-                to = target(t) * 8 + (my_place + i) % 8
-
-                @pl.when(to != me)
-                def _():
-                    act(to)
-
-                return inner
-
-            return lax.fori_loop(0, 8, one, carry)
-
-        lax.fori_loop(0, GROUPS, some, 0)
+            for i in range(8):
+                act((me + n // 2 + t * 8 + i) & (n - 1))
+            return carry
+
+        lax.fori_loop(0, n // 16, some, 0)
+        for i in range(1, 8):
+            act((me + i) & (n - 1))
+        lax.fori_loop(n // 16 + 1, n // 8, some, 0)
 
     barrier = pltpu.get_barrier_semaphore()
     each_other(lambda to: pl.semaphore_signal(barrier, 1, device_id={"dev": to}, device_id_type=MESH))
@@ -348,9 +344,6 @@
 
     prep_ids(rows_ref, lens_ref, counts_ref, ids_out)
     ids_in[me] = ids_out[me]
-    target_setup(inverse_ref, counts_ref, order_ref, compress_ref, turn_ref, mix_ref)
-    copies[0].wait()
-    pool_turn(tables_ref, turned_ref)
     pl.semaphore_wait(barrier, n - 1)
 
     def id_copy(src, dst, to):
@@ -360,19 +353,8 @@
         )
 
     each_other(lambda to: id_copy(ids_out.at[to], ids_in.at[me], to).start())
-    perm_ref[...] = order_columns(order_ref).astype(F32).T.astype(BF)
-    for g in range(GROUPS):
-        cols_ref[g] = mix_ref[:, g * 32 : g * 32 + 32]
-
-    def clear(g, carry):
-        rows = pl.ds(pl.multiple_of(arrived(GROUPS - 4 + g) * 32, 32), 32)
-        feat_ref[:, :, rows, :] = jnp.zeros((64, 2, 32, 128), BF)
-        return carry
-
-    def arrived(u):
-        return 2 * ((my_z + 8 - shift(u)) % 8) + (my_y + u) % 2
-
-    lax.fori_loop(0, 4, clear, 0)
+    copies[0].wait()
+    pool_turn(tables_ref, turned_ref)
     for copy in copies[1:]:
         copy.wait()
 
@@ -415,6 +397,20 @@
         return carry
 
     lax.fori_loop(0, GROUPS, step, 0)
+    target_setup(inverse_ref, counts_ref, order_ref, compress_ref, turn_ref, mix_ref)
+    perm_ref[...] = order_columns(order_ref).astype(F32).T.astype(BF)
+    for g in range(GROUPS):
+        cols_ref[g] = mix_ref[:, g * 32 : g * 32 + 32]
+
+    def clear(g, carry):
+        rows = pl.ds(pl.multiple_of(arrived(GROUPS - 4 + g) * 32, 32), 32)
+        feat_ref[:, :, rows, :] = jnp.zeros((64, 2, 32, 128), BF)
+        return carry
+
+    def arrived(u):
+        return 2 * ((my_z + 8 - shift(u)) % 8) + (my_y + u) % 2
+
+    lax.fori_loop(0, 4, clear, 0)
     mine = pl.ds(pl.multiple_of(me * ROOM, ROOM), ROOM)
     recv_ref[mine, :] = send_ref[mine, :]
 
@@ -506,15 +502,16 @@
             pltpu.SemaphoreType.DMA((2 * GROUPS,)),
         ]
     )
-    return pl.pallas_call(
+    hidden = pl.pallas_call(
         lookup_body,
-        out_shape=jax.ShapeDtypeStruct((samples, units), BF),
+        out_shape=jax.ShapeDtypeStruct((samples, units), F32),
         in_specs=[VM] * 7 + [anywhere] * 2,
         out_specs=VM,
         scratch_shapes=scratch,
         compiler_params=pltpu.CompilerParams(vmem_limit_bytes=BIG, collective_id=0, has_side_effects=True),
         cost_estimate=pl.CostEstimate(flops=3 * 10**10, bytes_accessed=16 << 20, transcendentals=0),
     )(rows, lens, row_counts, inverse, order, compress, bias, tables, top_weight)
+    return jnp.maximum(hidden, 0.0).astype(BF)
 
 
 def solution(mesh):

time: 104 us -> 101 us (0.971)
  Pallas kernels: 101 us -> 97.9 us
  other arithmetic: 0 us -> 1.63 us
  local copies, waits for them, and re-layouts: 1.57 us -> 0 us
    pallas_call x1, Pallas kernels: 101 us -> 97.9 us  [shards(): pl.pallas_call(lookup_body, out_shape=jax.ShapeDtypeStruct((samples, unit...]
    convert_element_type x0 -> x1, other arithmetic: none -> 1.63 us  [shards(): return jnp.maximum(hidden, 0.0).astype(BF)]
    unnamed x1 -> x0, local copies, waits for them, and re-layouts: 1.57 us -> none
where the time goes in v4:
time: 101 us; the launch traced here: 99.5 us
  Pallas kernels  97.9 us (97%)
  other arithmetic  1.63 us (2%)
    pallas_call x1, Pallas kernels, shards(): pl.pallas_call(lookup_body, out_shape=jax.ShapeDtypeStruct((samples, unit...  97.9 us

profile of v4, /device:TPU:8, one launch (start us, length us, event | category | flops | bytes accessed | tf_op | source)
XLA Modules:
  0.0 99.5 jit_solution(3952885839116187099)
XLA Ops:
  0.0 97.9 %shard_map.91 = f32[128,512]{1,0:T(8,128)} custom-call(s32[32,4,512]{2,1,0:T(4,128)} %bitcast.8, s32[32,512]{1,0:T(8,128)} %bitcast.9, s32[1,512]{1,0:T(1,128)} %counts_ref.1, s32[128,512]{1,0:T(8,128)} %inverse_ref.1, s32[1,512]{1,0:T(1,128)} %bitcast.10, bf16[16,512]{1,0:T(8,128)(2,1)} %compress_ref.1, f32[1,512]{1,0:T(1,128)} %bitcast.11, ...), custom_call_target="tpu_custom_call" | custom-call | flops 30000001024 | bytes 16777216 | tf_op jit(solution)/shard_map/pallas_call | solution.py:505
  97.9 1.6 %maximum_convert_fusion = bf16[128,512]{1,0:T(8,128)(2,1)} fusion(f32[128,512]{1,0:T(8,128)} %shard_map.91), kind=kLoop, calls=%fused_computation | loop fusion | flops 131072 | bytes 393216 | tf_op jit(solution)/shard_map/convert_element_type | solution.py:514

commit v5 on v4

--- a/solution.py
+++ b/solution.py
@@ -32,7 +32,7 @@
         ids_out[at * 32 : at * 32 + 32] = turned.astype(jnp.int16)
 
 
-PLANE = 512
+PLANE = 128
 
 
 def pool_turn(tables_ref, turned_ref):
@@ -45,10 +45,10 @@
 
 
 def pool_setup(load_ids, y_ref, code_ref, pos_ref, scale_ref):
-    lane = iota((32, 128), 1)
+    lane = iota((2, 128), 1)
     chunk = lane // 32
     same = onehot(iota((128, 128), 0) // 32 == iota((128, 128), 1) // 32)
-    base = jnp.zeros((32, 128), F32)
+    base = jnp.zeros((2, 128), F32)
     for j in range(4):
         got = [load_ids(q, j) for q in range(4)]
         ys = []
@@ -61,17 +61,18 @@
         valid = ys[0] >= 0
         total = jnp.dot(onehot(valid), same, preferred_element_type=F32)
         place = base.astype(I32) + (lane % 32) + chunk * ROOM
-        pos_ref[pl.ds(j * 32, 32), :] = jnp.where(valid, place, -1)
+        pos_ref[j * 8 : j * 8 + 2, :] = jnp.where(valid, place, -1)
         base = base + total
         alike = (ys[0] == ys[1]) & (ys[0] == ys[2]) & (ys[0] == ys[3])
-        scale_ref[pl.ds(j * 32, 32), :] = jnp.where(alike, 2.0, 1.0)
+        scale_ref[j * 8 : j * 8 + 2, :] = jnp.where(alike, 2.0, 1.0)
         for p in range(4):
             y = ys[p]
             live = (y >= 0) if p < 2 else ((y >= 0) & ~alike)
             code = jnp.where(live, jnp.left_shift(jnp.ones_like(y), ((y >> 7) * 2) & 31), 0)
-            y_ref[pl.ds((j * 4 + p) * 32, 32), :] = y & 127
+            at = (j * 4 + p) * 8
+            y_ref[at : at + 2, :] = y & 127
             for k in range(4):
-                code_ref[pl.ds(k * PLANE + (j * 4 + p) * 32, 32), :] = (
+                code_ref[k * PLANE + at : k * PLANE + at + 2, :] = (
                     lax.shift_right_logical(code, jnp.full_like(code, 8 * k)) & 255
                 )
 
@@ -80,10 +81,10 @@
     return jnp.broadcast_to(ref[pl.ds(at, 1), :], (16, 128)).astype(jnp.int16)
 
 
-def pool_table(t, j, turned_ref, y_ref, code_ref, scale_ref, xt_ref):
+def pool_table(j, turned_ref, y_ref, code_ref, scale_ref, xt_ref):
     low_iota = iota((16, 128), 0).astype(jnp.int16)
     zero = jnp.zeros((16, 128), jnp.int16)
-    rows = [[(j * 4 + p) * 32 + 2 * t + half for p in range(4)] for half in range(2)]
+    rows = [[(j * 4 + p) * 8 + half for p in range(4)] for half in range(2)]
     hits = []
     for half in range(2):
         lows = [small(y_ref, row) for row in rows[half]]
@@ -110,18 +111,18 @@
             part = jnp.dot(left, hot, preferred_element_type=F32)
             total = part if total is None else total + part
     for half in range(2):
-        scale = scale_ref[pl.ds(j * 32 + 2 * t + half, 1), :]
+        scale = scale_ref[pl.ds(j * 8 + half, 1), :]
         xt_ref[half, j] = (total[:, half * 128 : half * 128 + 128] * scale).astype(BF)
 
 
-def pool_pack(t, pos_ref, xt_ref):
+def pool_pack(pos_ref, xt_ref):
     out = []
     for half in range(2):
         total = None
         for jj in range(2):
             packs, cols = [], []
             for j in (2 * jj, 2 * jj + 1):
-                pos = small(pos_ref, j * 32 + 2 * t + half)
+                pos = small(pos_ref, j * 8 + half)
                 hits = [
                     jnp.where(
                         pos == iota((16, 128), 0).astype(jnp.int16) + jnp.int16(16 * at),
@@ -143,19 +144,13 @@
     return out
 
 
-def pool_step(t, turned_ref, y_ref, code_ref, pos_ref, scale_ref, xt_ref):
-    for j in range(4):
-        pool_table(t, j, turned_ref, y_ref, code_ref, scale_ref, xt_ref)
-    return pool_pack(t, pos_ref, xt_ref)
-
-
 def pool_scratch():
     return [
         pltpu.VMEM((4, 16, 128, 128), BF),
         pltpu.VMEM((PLANE, 128), I32),
         pltpu.VMEM((4 * PLANE, 128), I32),
-        pltpu.VMEM((128, 128), I32),
-        pltpu.VMEM((128, 128), F32),
+        pltpu.VMEM((32, 128), I32),
+        pltpu.VMEM((32, 128), F32),
         pltpu.VMEM((2, 4, 128, 128), BF),
     ]
 
@@ -238,36 +233,36 @@
 
 def mixing(columns, feats_of, store):
     def some(i, carry):
-        for u in range(8):
-            feats = jnp.concatenate([feats_of(i * 8 + u, v) for v in range(2)], axis=1)
-            store(i * 8 + u, jnp.dot(columns, feats, preferred_element_type=F32))
-        return carry
-
-    lax.fori_loop(0, 8, some, 0)
+        for u in range(16):
+            feats = jnp.concatenate([feats_of(i * 16 + u, v) for v in range(2)], axis=1)
+            store(i * 16 + u, jnp.dot(columns, feats, preferred_element_type=F32))
+        return carry
+
+    lax.fori_loop(0, 4, some, 0)
 
 
 def finish(feat_ref, weight_at, bias_ref, out_ref, left_ref, pair_ref, acc_ref):
     def pairing(i, carry):
-        for u in range(8):
+        for u in range(16):
             sides = [
-                jnp.concatenate([ref[i * 8 + u, v] for v in range(2)], axis=1) for ref in (left_ref, feat_ref)
+                jnp.concatenate([ref[i * 16 + u, v] for v in range(2)], axis=1) for ref in (left_ref, feat_ref)
             ]
             both = lax.dot_general(
                 sides[0], sides[1], (((1,), (1,)), ((), ())), preferred_element_type=F32
             )
             for v in range(2):
-                to = pl.ds(pl.multiple_of((v * 64 + i * 8 + u) * 24, 8), 16)
+                to = pl.ds(pl.multiple_of((v * 64 + i * 16 + u) * 24, 8), 16)
                 for at in range(4):
                     pair_ref[at, to, :] = both[v * 16 : v * 16 + 16, at * 128 : at * 128 + 128]
         return carry
 
-    lax.fori_loop(0, 8, pairing, 0)
+    lax.fori_loop(0, 4, pairing, 0)
     acc_ref[...] = jnp.broadcast_to(bias_ref[...], acc_ref.shape)
 
     def plane(i, carry):
         total = acc_ref[...]
-        for u in range(4):
-            k = i * 4 + u
+        for u in range(8):
+            k = i * 8 + u
             lhs = jnp.concatenate(
                 [pair_ref[at, pl.ds(k, 128, stride=24), :].astype(BF) for at in range(4)], axis=1
             )
@@ -276,7 +271,7 @@
         acc_ref[...] = total
         return carry
 
-    lax.fori_loop(0, 4, plane, 0)
+    lax.fori_loop(0, 2, plane, 0)
     out_ref[...] = acc_ref[...]
 
 
@@ -298,6 +293,10 @@
 
 MESH = pl.DeviceIdType.MESH
 GROUPS = 16
+ORDER = [(1, 0), (7, 0), (1, 1), (7, 1), (4, 0), (4, 1), (3, 0), (5, 0)]
+ORDER += [(3, 1), (5, 1), (0, 0), (0, 1), (2, 0), (6, 0), (2, 1), (6, 1)]
+SHIFTS = [sum(ORDER[8 * part + at][0] << (3 * at) for at in range(8)) for part in range(2)]
+HALVES = sum(dy << at for at, (_, dy) in enumerate(ORDER))
 
 
 def lookup_body(
@@ -313,14 +312,13 @@
     my_group, my_place, my_chunk = me // 8, me % 8, me // 4
     my_z, my_y = my_group // 2, my_group % 2
 
-    def shift(t):
-        m = t // 2
-        m = m - jnp.where(m > 3, 1, 0)
-        far = 4 + ((m + 1) // 2) * (1 - 2 * (m % 2))
-        return jnp.where(t // 2 == 3, 0, far)
+    def turn_of(t):
+        shifts = jnp.where(t < 8, SHIFTS[0], SHIFTS[1])
+        return (shifts >> (3 * (t & 7))) & 7, (HALVES >> t) & 1
 
     def target(t):
-        return 2 * ((my_z + shift(t)) % 8) + (my_y + t) % 2
+        dz, dy = turn_of(t)
+        return 2 * ((my_z + dz) & 7) + ((my_y + dy) & 1)
 
     def each_other(act):
         def some(t, carry):
@@ -346,24 +344,21 @@
     ids_in[me] = ids_out[me]
     pl.semaphore_wait(barrier, n - 1)
 
-    def id_copy(src, dst, to):
+    def id_copy(src, dst, to, group):
         return pltpu.make_async_remote_copy(
-            src_ref=src, dst_ref=dst, send_sem=ids_sems.at[0], recv_sem=ids_sems.at[1],
+            src_ref=src, dst_ref=dst, send_sem=send_sem.at[1], recv_sem=ids_sems.at[group],
             device_id={"dev": to}, device_id_type=MESH,
         )
 
-    each_other(lambda to: id_copy(ids_out.at[to], ids_in.at[me], to).start())
+    each_other(lambda to: id_copy(ids_out.at[to], ids_in.at[me], to, my_group).start())
     copies[0].wait()
     pool_turn(tables_ref, turned_ref)
     for copy in copies[1:]:
         copy.wait()
 
-    everyone = id_copy(ids_out.at[pl.ds(0, n - 1)], ids_in.at[pl.ds(0, n - 1)], (me + 1) % n)
-    everyone.wait_recv()
-    ids_wide[...] = ids_in[...].astype(I32)
-    pool_setup(
-        lambda q, j: ids_wide[pl.ds(q, 32, stride=4), j, :], y_ref, code_ref, pos_ref, scale_ref
-    )
+    def ids_of(group, count):
+        some = pl.ds(0, count)
+        return id_copy(ids_out.at[some], ids_in.at[some], (me + 1) % n, group)
 
     def row_copy(src, dst, to, chunk):
         return pltpu.make_async_remote_copy(
@@ -376,9 +371,22 @@
 
     def step(t, carry):
         group = target(t)
+
+        @pl.when(group == my_group)
+        def _():
+            ids_of(group, 7).wait_recv()
+
+        @pl.when(group != my_group)
+        def _():
+            ids_of(group, 8).wait_recv()
+
+        ids_wide[...] = ids_in[pl.ds(pl.multiple_of(group * 8, 8), 8)].astype(I32)
+        pool_setup(
+            lambda q, j: ids_wide[pl.ds(q, 2, stride=4), j, :], y_ref, code_ref, pos_ref, scale_ref
+        )
         for j in range(4):
-            pool_table(group, j, turned_ref, y_ref, code_ref, scale_ref, xt_ref)
-        blocks = pool_pack(group, pos_ref, xt_ref)
+            pool_table(j, turned_ref, y_ref, code_ref, scale_ref, xt_ref)
+        blocks = pool_pack(pos_ref, xt_ref)
         for half in range(2):
             send_ref[pl.ds(pl.multiple_of((2 * group + half) * 4 * ROOM, 4 * ROOM), 4 * ROOM), :] = blocks[half]
         for u in range(2):
@@ -408,46 +416,53 @@
         return carry
 
     def arrived(u):
-        return 2 * ((my_z + 8 - shift(u)) % 8) + (my_y + u) % 2
+        dz, dy = turn_of(u)
+        return 2 * ((my_z + 8 - dz) & 7) + ((my_y + dy) & 1)
 
     lax.fori_loop(0, 4, clear, 0)
     mine = pl.ds(pl.multiple_of(me * ROOM, ROOM), ROOM)
     recv_ref[mine, :] = send_ref[mine, :]
 
-    def take(u, carry):
-        group = arrived(u)
-
-        def half(v, inner):
-            chunk = 2 * group + (my_chunk + v) % 2
-
-            @pl.when(chunk == my_chunk)
-            def _():
-                rows = pl.ds(0, 3 * ROOM)
-                row_copy(send_ref.at[rows, :], recv_ref.at[rows, :], (me + 1) % n, chunk).wait_recv()
-
-            @pl.when(chunk != my_chunk)
-            def _():
-                rows = pl.ds(0, 4 * ROOM)
-                row_copy(send_ref.at[rows, :], recv_ref.at[rows, :], (me + 1) % n, chunk).wait_recv()
-
-            pick_chunk(chunk, recv_ref, turn_ref, feat_ref)
-            return inner
-
-        return lax.fori_loop(0, 2, half, carry)
-
-    def turn_and_take(u, carry):
-        for k in range(2):
-            weight_plane(2 * u + k, perm_ref, plane_ref, raw_ref)
-        return take(u, carry)
-
-    lax.fori_loop(0, 8, turn_and_take, 0)
-    lax.fori_loop(8, GROUPS - 4, take, 0)
+    def take(u, v):
+        chunk = 2 * arrived(u) + (my_chunk + v) % 2
+
+        @pl.when(chunk == my_chunk)
+        def _():
+            rows = pl.ds(0, 3 * ROOM)
+            row_copy(send_ref.at[rows, :], recv_ref.at[rows, :], (me + 1) % n, chunk).wait_recv()
+
+        @pl.when(chunk != my_chunk)
+        def _():
+            rows = pl.ds(0, 4 * ROOM)
+            row_copy(send_ref.at[rows, :], recv_ref.at[rows, :], (me + 1) % n, chunk).wait_recv()
+
+        pick_chunk(chunk, recv_ref, turn_ref, feat_ref)
+
+    def turn_and_take(w, carry):
+        weight_plane(w, perm_ref, plane_ref, raw_ref)
+        take(w // 2, w % 2)
+        return carry
+
+    def only_take(w, carry):
+        take(w // 2, w % 2)
+        return carry
+
+    def last_take(w, carry):
+        late = w // 4
+        take(
+            GROUPS - 4 + 2 * late + jnp.where(late == 1, w % 2, w // 2),
+            jnp.where(late == 1, (w - 4) // 2, w % 2),
+        )
+        return carry
+
+    lax.fori_loop(0, 16, turn_and_take, 0)
+    lax.fori_loop(16, 2 * GROUPS - 8, only_take, 0)
 
     def keep(i, value):
         sum_ref[i] = value
 
     mixing(mix_ref[...], lambda i, v: feat_ref[i, v], keep)
-    lax.fori_loop(GROUPS - 4, GROUPS, take, 0)
+    lax.fori_loop(0, 8, last_take, 0)
     last = [arrived(GROUPS - 4 + g) for g in range(4)]
     zero = jnp.zeros((16, 128), BF)
 
@@ -468,7 +483,7 @@
         feat_ref, lambda k, at: raw_ref[at, pl.ds(pl.multiple_of(k * 512, 512), 512), :],
         bias_ref, out_ref, left_ref, pair_ref, acc_ref,
     )
-    everyone.wait_send()
+    ids_of(my_group, n - 1).wait_send()
     rows = pl.ds(0, (n - 1) * ROOM)
     row_copy(send_ref.at[rows, :], recv_ref.at[rows, :], (me + 1) % n, my_chunk).wait_send()
 
@@ -489,7 +504,7 @@
             pltpu.VMEM((512, 512), BF),
             pltpu.VMEM((128, 4, 128), jnp.int16),
             pltpu.VMEM((128, 4, 128), jnp.int16),
-            pltpu.VMEM((128, 4, 128), I32),
+            pltpu.VMEM((8, 4, 128), I32),
             pltpu.VMEM((128 * ROOM, 128), BF),
             pltpu.VMEM((128 * ROOM, 128), BF),
         ]
@@ -497,8 +512,8 @@
         + [pltpu.VMEM((GROUPS, 16, 32), BF)]
         + [
             pltpu.SemaphoreType.DMA((5,)),
+            pltpu.SemaphoreType.DMA((GROUPS,)),
             pltpu.SemaphoreType.DMA((2,)),
-            pltpu.SemaphoreType.DMA((1,)),
             pltpu.SemaphoreType.DMA((2 * GROUPS,)),
         ]
     )

time: 101 us -> 95.4 us (0.945)
  the two profiles are of different devices: /device:TPU:8 before, /device:TPU:64 now
where the time goes in v5:
time: 95.4 us; the launch traced here: 95.3 us
  Pallas kernels  93.7 us (98%)
  other arithmetic  1.63 us (2%)
    pallas_call x1, Pallas kernels, shards(): pl.pallas_call(lookup_body, out_shape=jax.ShapeDtypeStruct((samples, unit...  93.7 us

profile of v5, /device:TPU:64, one launch (start us, length us, event | category | flops | bytes accessed | tf_op | source)
XLA Modules:
  0.0 95.3 jit_solution(13873705646706116022)
XLA Ops:
  0.0 93.7 %shard_map.91 = f32[128,512]{1,0:T(8,128)} custom-call(s32[32,4,512]{2,1,0:T(4,128)} %bitcast.8, s32[32,512]{1,0:T(8,128)} %bitcast.9, s32[1,512]{1,0:T(1,128)} %counts_ref.1, s32[128,512]{1,0:T(8,128)} %inverse_ref.1, s32[1,512]{1,0:T(1,128)} %bitcast.10, bf16[16,512]{1,0:T(8,128)(2,1)} %compress_ref.1, f32[1,512]{1,0:T(1,128)} %bitcast.11, ...), custom_call_target="tpu_custom_call" | custom-call | flops 30000001024 | bytes 16777216 | tf_op jit(solution)/shard_map/pallas_call | solution.py:520
  93.7 1.6 %maximum_convert_fusion = bf16[128,512]{1,0:T(8,128)(2,1)} fusion(f32[128,512]{1,0:T(8,128)} %shard_map.91), kind=kLoop, calls=%fused_computation | loop fusion | flops 131072 | bytes 393216 | tf_op jit(solution)/shard_map/convert_element_type | solution.py:529

commit v6 on v5

--- a/solution.py
+++ b/solution.py
@@ -243,20 +243,20 @@
 
 def finish(feat_ref, weight_at, bias_ref, out_ref, left_ref, pair_ref, acc_ref):
     def pairing(i, carry):
-        for u in range(16):
+        for u in range(32):
             sides = [
-                jnp.concatenate([ref[i * 16 + u, v] for v in range(2)], axis=1) for ref in (left_ref, feat_ref)
+                jnp.concatenate([ref[i * 32 + u, v] for v in range(2)], axis=1) for ref in (left_ref, feat_ref)
             ]
             both = lax.dot_general(
                 sides[0], sides[1], (((1,), (1,)), ((), ())), preferred_element_type=F32
             )
             for v in range(2):
-                to = pl.ds(pl.multiple_of((v * 64 + i * 16 + u) * 24, 8), 16)
+                to = pl.ds(pl.multiple_of((v * 64 + i * 32 + u) * 24, 8), 16)
                 for at in range(4):
                     pair_ref[at, to, :] = both[v * 16 : v * 16 + 16, at * 128 : at * 128 + 128]
         return carry
 
-    lax.fori_loop(0, 4, pairing, 0)
+    lax.fori_loop(0, 2, pairing, 0)
     acc_ref[...] = jnp.broadcast_to(bias_ref[...], acc_ref.shape)
 
     def plane(i, carry):
@@ -293,10 +293,12 @@
 
 MESH = pl.DeviceIdType.MESH
 GROUPS = 16
-ORDER = [(1, 0), (7, 0), (1, 1), (7, 1), (4, 0), (4, 1), (3, 0), (5, 0)]
-ORDER += [(3, 1), (5, 1), (0, 0), (0, 1), (2, 0), (6, 0), (2, 1), (6, 1)]
+ORDER = [(1, 0), (1, 1)] + [(4, y) for y in range(4)] + [(3, y) for y in range(4)] + [(2, y) for y in range(4)]
+ORDER += [(1, 2), (1, 3)]
 SHIFTS = [sum(ORDER[8 * part + at][0] << (3 * at) for at in range(8)) for part in range(2)]
-HALVES = sum(dy << at for at, (_, dy) in enumerate(ORDER))
+SIDES = sum(dy << (2 * at) for at, (_, dy) in enumerate(ORDER[:15]))
+NEAR = [13, 14, 1, 2, 12, 15, 3, 4, 11, 5, 10, 6, 9, 7, 8]
+NEARS = [sum(part[at] << (4 * at) for at in range(len(part))) for part in (NEAR[:7], NEAR[7:14])]
 
 
 def lookup_body(
@@ -309,16 +311,21 @@
 ):
     n = 8 * GROUPS
     me = lax.axis_index("dev")
-    my_group, my_place, my_chunk = me // 8, me % 8, me // 4
-    my_z, my_y = my_group // 2, my_group % 2
-
-    def turn_of(t):
-        shifts = jnp.where(t < 8, SHIFTS[0], SHIFTS[1])
-        return (shifts >> (3 * (t & 7))) & 7, (HALVES >> t) & 1
-
-    def target(t):
-        dz, dy = turn_of(t)
-        return 2 * ((my_z + dz) & 7) + ((my_y + dy) & 1)
+    my_place, my_chunk = me & 3, me // 4
+    my_z, my_y = my_chunk // 4, my_chunk & 3
+
+    def turn_of(t, half):
+        dz = (jnp.where(t < 8, SHIFTS[0], SHIFTS[1]) >> (3 * (t & 7))) & 7
+        dy = jnp.where(t == GROUPS - 1, ORDER[-1][1], (SIDES >> (2 * jnp.minimum(t, GROUPS - 2))) & 3)
+        return jnp.where(half == 0, dz, jnp.where(dz == 4, 0, 8 - dz)), dy
+
+    def target(t, half):
+        dz, dy = turn_of(t, half)
+        return 4 * ((my_z + dz) & 7) + ((my_y + dy) & 3)
+
+    def arrived(t, half):
+        dz, dy = turn_of(t, half)
+        return 4 * ((my_z + 8 - dz) & 7) + ((my_y + 4 - dy) & 3)
 
     def each_other(act):
         def some(t, carry):
@@ -330,6 +337,19 @@
         for i in range(1, 8):
             act((me + i) & (n - 1))
         lax.fori_loop(n // 16 + 1, n // 8, some, 0)
+
+    def near_first(act):
+        def some(t, carry):
+            at = (jnp.where(t < 7, NEARS[0], NEARS[1]) >> (4 * jnp.where(t < 7, t, t - 7))) & 15
+            for i in range(8):
+                act((me + at * 8 + i) & (n - 1))
+            return carry
+
+        lax.fori_loop(0, 14, some, 0)
+        for i in range(1, 8):
+            act((me + i) & (n - 1))
+        for i in range(8):
+            act((me + NEAR[14] * 8 + i) & (n - 1))
 
     barrier = pltpu.get_barrier_semaphore()
     each_other(lambda to: pl.semaphore_signal(barrier, 1, device_id={"dev": to}, device_id_type=MESH))
@@ -350,7 +370,7 @@
             device_id={"dev": to}, device_id_type=MESH,
         )
 
-    each_other(lambda to: id_copy(ids_out.at[to], ids_in.at[me], to, my_group).start())
+    near_first(lambda to: id_copy(ids_out.at[to], ids_in.at[me], to, my_chunk).start())
     copies[0].wait()
     pool_turn(tables_ref, turned_ref)
     for copy in copies[1:]:
@@ -369,18 +389,22 @@
     def block(ref, device):
         return ref.at[pl.ds(pl.multiple_of(device * ROOM, ROOM), ROOM), :]
 
+    def wait_ids(chunk):
+        @pl.when(chunk == my_chunk)
+        def _():
+            ids_of(chunk, 3).wait_recv()
+
+        @pl.when(chunk != my_chunk)
+        def _():
+            ids_of(chunk, 4).wait_recv()
+
     def step(t, carry):
-        group = target(t)
-
-        @pl.when(group == my_group)
-        def _():
-            ids_of(group, 7).wait_recv()
-
-        @pl.when(group != my_group)
-        def _():
-            ids_of(group, 8).wait_recv()
-
-        ids_wide[...] = ids_in[pl.ds(pl.multiple_of(group * 8, 8), 8)].astype(I32)
+        chunks = [target(t, half) for half in range(2)]
+        for half in range(2):
+            wait_ids(chunks[half])
+            ids_wide[half * 4 : half * 4 + 4] = ids_in[
+                pl.ds(pl.multiple_of(chunks[half] * 4, 4), 4)
+            ].astype(I32)
         pool_setup(
             lambda q, j: ids_wide[pl.ds(q, 2, stride=4), j, :], y_ref, code_ref, pos_ref, scale_ref
         )
@@ -388,43 +412,37 @@
             pool_table(j, turned_ref, y_ref, code_ref, scale_ref, xt_ref)
         blocks = pool_pack(pos_ref, xt_ref)
         for half in range(2):
-            send_ref[pl.ds(pl.multiple_of((2 * group + half) * 4 * ROOM, 4 * ROOM), 4 * ROOM), :] = blocks[half]
+            send_ref[pl.ds(pl.multiple_of(chunks[half] * 4 * ROOM, 4 * ROOM), 4 * ROOM), :] = blocks[half]
         for u in range(2):
             weight_cut(2 * t + u, raw_ref, plane_ref)
 
-        def one(i, inner):
-            to = group * 8 + (my_place + i) % 8
-
-            @pl.when(to != me)
-            def _():
-                row_copy(block(send_ref, to), block(recv_ref, me), to, my_chunk).start()
-
-            return inner
-
-        lax.fori_loop(0, 8, one, 0)
+        for i in range(4):
+            for half in range(2):
+                to = chunks[half] * 4 + ((my_place + i) & 3)
+
+                @pl.when(to != me)
+                def _():
+                    row_copy(block(send_ref, to), block(recv_ref, me), to, my_chunk).start()
+
         return carry
 
     lax.fori_loop(0, GROUPS, step, 0)
     target_setup(inverse_ref, counts_ref, order_ref, compress_ref, turn_ref, mix_ref)
     perm_ref[...] = order_columns(order_ref).astype(F32).T.astype(BF)
-    for g in range(GROUPS):
-        cols_ref[g] = mix_ref[:, g * 32 : g * 32 + 32]
-
-    def clear(g, carry):
-        rows = pl.ds(pl.multiple_of(arrived(GROUPS - 4 + g) * 32, 32), 32)
-        feat_ref[:, :, rows, :] = jnp.zeros((64, 2, 32, 128), BF)
-        return carry
-
-    def arrived(u):
-        dz, dy = turn_of(u)
-        return 2 * ((my_z + 8 - dz) & 7) + ((my_y + dy) & 1)
-
-    lax.fori_loop(0, 4, clear, 0)
+    for c in range(2 * GROUPS):
+        cols_ref[c] = mix_ref[:, c * 16 : c * 16 + 16]
+
+    def clear(w, carry):
+        rows = pl.ds(pl.multiple_of(arrived(GROUPS - 4 + w // 2, w % 2) * 16, 16), 16)
+        feat_ref[:, :, rows, :] = jnp.zeros((64, 2, 16, 128), BF)
+        return carry
+
+    lax.fori_loop(0, 8, clear, 0)
     mine = pl.ds(pl.multiple_of(me * ROOM, ROOM), ROOM)
     recv_ref[mine, :] = send_ref[mine, :]
 
     def take(u, v):
-        chunk = 2 * arrived(u) + (my_chunk + v) % 2
+        chunk = arrived(u, v)
 
         @pl.when(chunk == my_chunk)
         def _():
@@ -447,14 +465,6 @@
         take(w // 2, w % 2)
         return carry
 
-    def last_take(w, carry):
-        late = w // 4
-        take(
-            GROUPS - 4 + 2 * late + jnp.where(late == 1, w % 2, w // 2),
-            jnp.where(late == 1, (w - 4) // 2, w % 2),
-        )
-        return carry
-
     lax.fori_loop(0, 16, turn_and_take, 0)
     lax.fori_loop(16, 2 * GROUPS - 8, only_take, 0)
 
@@ -462,8 +472,8 @@
         sum_ref[i] = value
 
     mixing(mix_ref[...], lambda i, v: feat_ref[i, v], keep)
-    lax.fori_loop(0, 8, last_take, 0)
-    last = [arrived(GROUPS - 4 + g) for g in range(4)]
+    lax.fori_loop(2 * GROUPS - 8, 2 * GROUPS, only_take, 0)
+    last = [arrived(GROUPS - 4 + w // 2, w % 2) for w in range(8)]
     zero = jnp.zeros((16, 128), BF)
 
     def settle(i, value):
@@ -473,9 +483,9 @@
             left_ref[i, v, 16 - v * 16 : 32 - v * 16, :] = zero
 
     mixing(
-        jnp.concatenate([cols_ref[g] for g in last], axis=1),
+        jnp.concatenate([cols_ref[c] for c in last], axis=1),
         lambda i, v: jnp.concatenate(
-            [feat_ref[i, v, pl.ds(pl.multiple_of(g * 32, 32), 32), :] for g in last], axis=0
+            [feat_ref[i, v, pl.ds(pl.multiple_of(c * 16, 16), 16), :] for c in last], axis=0
         ),
         settle,
     )
@@ -483,7 +493,7 @@
         feat_ref, lambda k, at: raw_ref[at, pl.ds(pl.multiple_of(k * 512, 512), 512), :],
         bias_ref, out_ref, left_ref, pair_ref, acc_ref,
     )
-    ids_of(my_group, n - 1).wait_send()
+    ids_of(my_chunk, n - 1).wait_send()
     rows = pl.ds(0, (n - 1) * ROOM)
     row_copy(send_ref.at[rows, :], recv_ref.at[rows, :], (me + 1) % n, my_chunk).wait_send()
 
@@ -509,10 +519,10 @@
             pltpu.VMEM((128 * ROOM, 128), BF),
         ]
         + score_scratch()
-        + [pltpu.VMEM((GROUPS, 16, 32), BF)]
+        + [pltpu.VMEM((2 * GROUPS, 16, 16), BF)]
         + [
             pltpu.SemaphoreType.DMA((5,)),
-            pltpu.SemaphoreType.DMA((GROUPS,)),
+            pltpu.SemaphoreType.DMA((2 * GROUPS,)),
             pltpu.SemaphoreType.DMA((2,)),
             pltpu.SemaphoreType.DMA((2 * GROUPS,)),
         ]

time: 95.4 us -> 93.7 us (0.982)
  the two profiles are of different devices: /device:TPU:64 before, /device:TPU:8 now
where the time goes in v6:
time: 93.7 us; the launch traced here: 93.6 us
  Pallas kernels  91.9 us (98%)
  other arithmetic  1.63 us (2%)
    pallas_call x1, Pallas kernels, shards(): pl.pallas_call(lookup_body, out_shape=jax.ShapeDtypeStruct((samples, unit...  91.9 us

profile of v6, /device:TPU:8, one launch (start us, length us, event | category | flops | bytes accessed | tf_op | source)
XLA Modules:
  0.0 93.6 jit_solution(5781322987381446056)
XLA Ops:
  0.0 91.9 %shard_map.91 = f32[128,512]{1,0:T(8,128)} custom-call(s32[32,4,512]{2,1,0:T(4,128)} %bitcast.8, s32[32,512]{1,0:T(8,128)} %bitcast.9, s32[1,512]{1,0:T(1,128)} %counts_ref.1, s32[128,512]{1,0:T(8,128)} %inverse_ref.1, s32[1,512]{1,0:T(1,128)} %bitcast.10, bf16[16,512]{1,0:T(8,128)(2,1)} %compress_ref.1, f32[1,512]{1,0:T(1,128)} %bitcast.11, ...), custom_call_target="tpu_custom_call" | custom-call | flops 30000001024 | bytes 16777216 | tf_op jit(solution)/shard_map/pallas_call | solution.py:530
  92.0 1.6 %maximum_convert_fusion = bf16[128,512]{1,0:T(8,128)(2,1)} fusion(f32[128,512]{1,0:T(8,128)} %shard_map.91), kind=kLoop, calls=%fused_computation | loop fusion | flops 131072 | bytes 393216 | tf_op jit(solution)/shard_map/convert_element_type | solution.py:539

commit v7 on v6

--- a/solution.py
+++ b/solution.py
@@ -302,8 +302,9 @@
 
 
 def lookup_body(
-    rows_ref, lens_ref, counts_ref, inverse_ref, order_ref, compress_ref, bias_ref, tables_hbm, top_hbm,
+    rows_hbm, lens_hbm, counts_hbm, inverse_hbm, order_hbm, compress_hbm, bias_hbm, tables_hbm, top_hbm,
     out_ref,
+    rows_ref, lens_ref, counts_ref, inverse_ref, order_ref, compress_ref, bias_ref,
     tables_ref, turned_ref, y_ref, code_ref, pos_ref, scale_ref, xt_ref,
     raw_ref, plane_ref, perm_ref, ids_out, ids_in, ids_wide, send_ref, recv_ref,
     turn_ref, mix_ref, feat_ref, left_ref, sum_ref, pair_ref, acc_ref, cols_ref,
@@ -351,6 +352,17 @@
         for i in range(8):
             act((me + NEAR[14] * 8 + i) & (n - 1))
 
+    small_copies = [
+        pltpu.make_async_copy(src, dst, local_sems.at[5 + at])
+        for at, (src, dst) in enumerate(
+            (
+                (rows_hbm, rows_ref), (lens_hbm, lens_ref), (counts_hbm, counts_ref), (inverse_hbm, inverse_ref),
+                (order_hbm, order_ref), (compress_hbm, compress_ref), (bias_hbm, bias_ref),
+            )
+        )
+    ]
+    for copy in small_copies:
+        copy.start()
     barrier = pltpu.get_barrier_semaphore()
     each_other(lambda to: pl.semaphore_signal(barrier, 1, device_id={"dev": to}, device_id_type=MESH))
     copies = [pltpu.make_async_copy(tables_hbm, tables_ref, local_sems.at[4])] + [
@@ -360,6 +372,8 @@
     for copy in copies:
         copy.start()
 
+    for copy in small_copies[:3]:
+        copy.wait()
     prep_ids(rows_ref, lens_ref, counts_ref, ids_out)
     ids_in[me] = ids_out[me]
     pl.semaphore_wait(barrier, n - 1)
@@ -373,7 +387,7 @@
     near_first(lambda to: id_copy(ids_out.at[to], ids_in.at[me], to, my_chunk).start())
     copies[0].wait()
     pool_turn(tables_ref, turned_ref)
-    for copy in copies[1:]:
+    for copy in copies[1:] + small_copies[3:]:
         copy.wait()
 
     def ids_of(group, count):
@@ -506,7 +520,8 @@
     samples, units = inverse.shape[0], top_weight.shape[1]
     anywhere = pl.BlockSpec(memory_space=pl.ANY)
     scratch = (
-        [pltpu.VMEM(tables.shape, BF)]
+        [pltpu.VMEM(x.shape, x.dtype) for x in (rows, lens, row_counts, inverse, order, compress, bias)]
+        + [pltpu.VMEM(tables.shape, BF)]
         + pool_scratch()
         + [
             pltpu.VMEM((units // 128, top_weight.shape[0], 128), BF),
@@ -521,7 +536,7 @@
         + score_scratch()
         + [pltpu.VMEM((2 * GROUPS, 16, 16), BF)]
         + [
-            pltpu.SemaphoreType.DMA((5,)),
+            pltpu.SemaphoreType.DMA((12,)),
             pltpu.SemaphoreType.DMA((2 * GROUPS,)),
             pltpu.SemaphoreType.DMA((2,)),
             pltpu.SemaphoreType.DMA((2 * GROUPS,)),
@@ -530,7 +545,7 @@
     hidden = pl.pallas_call(
         lookup_body,
         out_shape=jax.ShapeDtypeStruct((samples, units), F32),
-        in_specs=[VM] * 7 + [anywhere] * 2,
+        in_specs=[anywhere] * 9,
         out_specs=VM,
         scratch_shapes=scratch,
         compiler_params=pltpu.CompilerParams(vmem_limit_bytes=BIG, collective_id=0, has_side_effects=True),

time: 93.7 us -> 92.8 us (level)
    pallas_call x1, Pallas kernels: 91.9 us -> 91 us  [shards(): pl.pallas_call(lookup_body, out_shape=jax.ShapeDtypeStruct((samples, unit...]
where the time goes in v7:
time: 92.8 us; the launch traced here: 92.6 us
  Pallas kernels  91 us (98%)
  other arithmetic  1.63 us (2%)
    pallas_call x1, Pallas kernels, shards(): pl.pallas_call(lookup_body, out_shape=jax.ShapeDtypeStruct((samples, unit...  91 us

profile of v7, /device:TPU:8, one launch (start us, length us, event | category | flops | bytes accessed | tf_op | source)
XLA Modules:
  0.0 92.6 jit_solution(11759697252791620209)
XLA Ops:
  0.0 91.0 %shard_map.91 = f32[128,512]{1,0:T(8,128)} custom-call(s32[32,4,512]{2,1,0:T(4,128)} %bitcast.8, s32[32,512]{1,0:T(8,128)} %bitcast.9, s32[1,512]{1,0:T(1,128)} %counts_hbm.1, s32[128,512]{1,0:T(8,128)} %inverse_hbm.1, s32[1,512]{1,0:T(1,128)} %bitcast.10, bf16[16,512]{1,0:T(8,128)(2,1)} %compress_hbm.1, f32[1,512]{1,0:T(1,128)} %bitcast.11, ...), custom_call_target="tpu_custom_call" | custom-call | flops 30000001024 | bytes 16777216 | tf_op jit(solution)/shard_map/pallas_call | solution.py:545
  91.0 1.6 %maximum_convert_fusion = bf16[128,512]{1,0:T(8,128)(2,1)} fusion(f32[128,512]{1,0:T(8,128)} %shard_map.91), kind=kLoop, calls=%fused_computation | loop fusion | flops 131072 | bytes 393216 | tf_op jit(solution)/shard_map/convert_element_type | solution.py:554

commit v8 on v7

--- a/solution.py
+++ b/solution.py
@@ -282,7 +282,7 @@
         pltpu.VMEM((64, 2, 512, 128), BF),
         pltpu.VMEM((64, 2, 32, 128), BF),
         pltpu.VMEM((64, 16, 256), F32),
-        pltpu.VMEM((4, 3072, 128), F32),
+        pltpu.VMEM((4, 3200, 128), F32),
         pltpu.VMEM((128, 512), F32),
     ]
 
@@ -529,7 +529,7 @@
             pltpu.VMEM((512, 512), BF),
             pltpu.VMEM((128, 4, 128), jnp.int16),
             pltpu.VMEM((128, 4, 128), jnp.int16),
-            pltpu.VMEM((8, 4, 128), I32),
+            pltpu.VMEM((16, 4, 128), I32),
             pltpu.VMEM((128 * ROOM, 128), BF),
             pltpu.VMEM((128 * ROOM, 128), BF),
         ]

time: 92.8 us -> 92.7 us (level)
  no operation moved by 1% of the time
where the time goes in v8:
time: 92.7 us; the launch traced here: 92.6 us
  Pallas kernels  91 us (98%)
  other arithmetic  1.63 us (2%)
    pallas_call x1, Pallas kernels, shards(): pl.pallas_call(lookup_body, out_shape=jax.ShapeDtypeStruct((samples, unit...  91 us

profile of v8, /device:TPU:8, one launch (start us, length us, event | category | flops | bytes accessed | tf_op | source)
XLA Modules:
  0.0 92.6 jit_solution(18013616600354841044)
XLA Ops:
  0.0 91.0 %shard_map.91 = f32[128,512]{1,0:T(8,128)} custom-call(s32[32,4,512]{2,1,0:T(4,128)} %bitcast.8, s32[32,512]{1,0:T(8,128)} %bitcast.9, s32[1,512]{1,0:T(1,128)} %counts_hbm.1, s32[128,512]{1,0:T(8,128)} %inverse_hbm.1, s32[1,512]{1,0:T(1,128)} %bitcast.10, bf16[16,512]{1,0:T(8,128)(2,1)} %compress_hbm.1, f32[1,512]{1,0:T(1,128)} %bitcast.11, ...), custom_call_target="tpu_custom_call" | custom-call | flops 30000001024 | bytes 16777216 | tf_op jit(solution)/shard_map/pallas_call | solution.py:545
  91.0 1.6 %maximum_convert_fusion = bf16[128,512]{1,0:T(8,128)(2,1)} fusion(f32[128,512]{1,0:T(8,128)} %shard_map.91), kind=kLoop, calls=%fused_computation | loop fusion | flops 131072 | bytes 393216 | tf_op jit(solution)/shard_map/convert_element_type | solution.py:554
